TPU v7x, 128 devices: a whole 4x4x4 slice. The times are simulated.
128 devices in a mesh: bx: 16 (over x, z_lo, core), by: 8 (over z_hi, y).
Axes of the slice: x: 4, y: 4, z: 4 (z_hi: 2, z_lo: 2; z = z_hi * 2 + z_lo), core: 2. Of those that a mesh axis runs over, the one named last changes fastest.
Arguments:
- photon_data: float32 [6, 1024, 256, 128], P(None, 'bx', 'by'), may hold values from 0 to 1, as said below
- block_counts: int32 [1024, 256], P('bx', 'by'), may hold values from 1 to 128
- gather_offsets: float32 [3, 524288], P(None, ('bx', 'by')), may hold values from 0 to 1, as said below
- gather_blocks: int32 [4, 524288], P(None, ('bx', 'by')), may hold values from 0 to 262143, as said below
- albedo: float32 [3, 524288], P(None, ('bx', 'by')), may hold values from 0.1 to 1
- gather_pixels: int32 [524288], P(('bx', 'by')), may hold values from 0 to 262143, as said below
- tile_slot: int32 [1024], replicated, may hold values from 0 to 1023, as said below
Outputs:
- film: float32 [3, 1024, 256], P(None, ('bx', 'by'))
Inputs may be any that keep to these rules, and one draw needn't show every extreme that they name: `photon_data`: per point and channel in cell units: entries 0 to 2 are a position in [0, 1), entries 3 to 5 a positive power. `gather_offsets`: each coordinate lies in [0, 1). `gather_blocks`: entry 0 is the point's own cell, inside the brick of the device that holds the point; the 4 entries are the four different cells of a 2 x 2 square of cells (periodic) that contains it. `gather_pixels`: in the rows of one device, at most 96 gather points lie in tiles whose slots s share s // 8; in every draw some such owner group receives exactly 96 from every device. `tile_slot`: A permutation of 0 to 1023.
All inputs are finite; a program needn't handle non-finite values.
Results may differ from a plain program's by a relative error of at most 0.0003.
Values sent between devices are 32-bit elements; how exact they have to be, the bound alone decides.
A program may use at most 512 MiB of HBM per device.

v0:
```python
import jax
import jax.numpy as jnp
from jax import lax
from jax.sharding import Mesh
from jax.sharding import PartitionSpec as P

TILE_PIX = 256
BX = ("bx_0", "bx_1", "bx_2")
BY = ("by_0", "by_1")
BX_BY = ("bx_0", "bx_1", "bx_2", "by_0", "by_1")


RADIUS_SQ = 0.25


def extended(x, sides, width):
    for axis, dim in sides:
        peers, length = (lax.axis_size(axis), x.shape[dim])
        up = [(i, (i + 1) % peers) for i in range(peers)]
        down = [(j, i) for i, j in up]
        last = lax.slice_in_dim(x, length - width, length, axis=dim)
        initial = lax.slice_in_dim(x, 0, width, axis=dim)
        before = lax.ppermute(last, axis, up)
        after = lax.ppermute(initial, axis, down)
        x = jnp.concatenate([before, x, after], axis=dim)
    return x


def cut_along(x, dim, peers):
    before, after = (x.shape[:dim], x.shape[dim + 1 :])
    return jnp.moveaxis(x.reshape(*before, peers, -1, *after), dim, 0)


def edges_of(length, count):
    turn = length // count
    if turn >= 8:
        turn -= turn % 8
    return [turn * k for k in range(1, count)]


def sum_in_order(blocks, axes, sequence):
    inside = blocks.shape[1:]
    blocks = blocks.reshape(*(lax.axis_size(a) for a in axes), *inside)
    blocks = jnp.moveaxis(blocks, sequence, range(len(axes))).reshape(-1, *inside)
    for k in sequence:
        blocks = lax.psum_scatter(blocks, axes[k], scatter_dimension=0, tiled=True)
    return blocks[0]


def sum_all_axes(x, axes, dim):
    blocks = cut_along(x, dim, lax.axis_size(axes))
    cut = max(range(1, max(2, blocks.ndim - 1)), key=lambda d: blocks.shape[d])
    count, finished = (len(axes), [])
    for initial, share in enumerate(
        jnp.split(blocks, edges_of(blocks.shape[cut], count), axis=cut)
    ):
        if share.size:
            sequence = [(initial + k) % count for k in range(count)]
            finished.append(sum_in_order(share, axes, sequence))
    return jnp.concatenate(finished, axis=cut - 1)


def kernel_sum(blocks, shift_x, shift_y, offsets, albedo):
    delta_x = shift_x[:, :, None] + blocks[0] - offsets[0][:, None, None]
    delta_y = shift_y[:, :, None] + blocks[1] - offsets[1][:, None, None]
    delta_z = blocks[2] - offsets[2][:, None, None]
    dist_sq = delta_x * delta_x + delta_y * delta_y + delta_z * delta_z
    weight = jnp.maximum(1.0 - dist_sq / RADIUS_SQ, 0.0)
    sums = jnp.sum(weight[None] * blocks[3:6], axis=(2, 3))
    return albedo * sums


def per_device(
    photon_data, block_counts, gather_offsets, gather_blocks, albedo, gather_pixels, tile_slot
):
    cells_x, cells_y, slots = (photon_data.shape[1], photon_data.shape[2], photon_data.shape[3])
    span_x = lax.axis_size(BX)
    span_y = lax.axis_size(BY)
    grid_x = cells_x * span_x
    grid_y = cells_y * span_y
    occupied = (
        lax.broadcasted_iota(jnp.int32, (cells_x, cells_y, slots), 2) < block_counts[:, :, None]
    )
    photons = jnp.concatenate(
        [photon_data[:3], photon_data[3:] * occupied.astype(jnp.float32)[None]], axis=0
    )
    padded = extended(photons, ((BX, 1), (BY, 2)), 1)
    table = padded.reshape(6, (cells_x + 2) * (cells_y + 2), slots)
    first_x = lax.axis_index(BX) * cells_x
    first_y = lax.axis_index(BY) * cells_y
    local_x = (gather_blocks // grid_y - first_x + 1) % grid_x
    local_y = (gather_blocks % grid_y - first_y + 1) % grid_y
    shift_x = (local_x - local_x[:1]).astype(jnp.float32)
    shift_y = (local_y - local_y[:1]).astype(jnp.float32)
    index = local_x * (cells_y + 2) + local_y
    listed = gather_blocks.shape[0]
    points = gather_offsets.shape[1]
    group = min(512, points)
    groups = points // group
    idx_stack = index.reshape(listed, groups, group).transpose(1, 2, 0)
    sx_stack = shift_x.reshape(listed, groups, group).transpose(1, 2, 0)
    sy_stack = shift_y.reshape(listed, groups, group).transpose(1, 2, 0)
    off_stack = gather_offsets.reshape(3, groups, group).transpose(1, 0, 2)
    alb_stack = albedo.reshape(3, groups, group).transpose(1, 0, 2)

    def one_group(packed):
        idb, move_x, move_y, off, alb = packed
        blocks = jnp.take(table, idb.reshape(-1), axis=1).reshape(6, group, listed, slots)
        return kernel_sum(blocks, move_x, move_y, off, alb)

    rad = lax.map(one_group, (idx_stack, sx_stack, sy_stack, off_stack, alb_stack))
    radiance = rad.transpose(1, 0, 2).reshape(3, points)
    tiles = tile_slot.shape[0]
    tile = gather_pixels // TILE_PIX
    matched = tile[:, None] == jnp.arange(tiles, dtype=jnp.int32)[None, :]
    slot = jnp.sum(jnp.where(matched, tile_slot[None, :], 0), axis=1)
    within_tile = gather_pixels % TILE_PIX
    target = slot * TILE_PIX + within_tile
    partial_film = jnp.zeros((3, tiles * TILE_PIX), jnp.float32).at[:, target].add(radiance)
    partial_film = partial_film.reshape(3, tiles, TILE_PIX)
    return sum_all_axes(partial_film, BX_BY, 1)


def solution(mesh):
    split = Mesh(mesh.devices.reshape(4, 2, 2, 2, 4), ("bx_0", "bx_1", "bx_2", "by_0", "by_1"))
    in_specs = (
        P(None, BX, BY, None),
        P(BX, BY),
        P(None, BX_BY),
        P(None, BX_BY),
        P(None, BX_BY),
        P(BX_BY),
        P(),
    )
    out_specs = P(None, BX_BY, None)
    return jax.shard_map(
        per_device, mesh=split, in_specs=in_specs, out_specs=out_specs, check_vma=False
    )
```

profile of v0, /device:TPU:1, one launch (start us, length us, event | category | flops | bytes accessed | tf_op | source)
XLA Modules:
  0.0 1016.2 jit_solution(8119169532902245180)
XLA Ops:
  7.7 3.7 fusion.24
  13.8 3.0 collective-permute-start
  17.1 3.7 select_reduce_fusion
  27.5 5.7 sort
  36.5 4.7 collective-permute-start.3
  41.3 3.0 collective-permute-done.2
  44.8 3.1 pad_maximum_fusion
  47.9 5.8 copy.92
  53.7 412.1 %while.10 = (s32[]{:T(128)}, f32[8,3,512]{2,1,0:T(4,128)S(1)}, f32[8,3,512]{2,1,0:T(4,128)}, f32[8,512,4]{2,1,0:T(8,128)}, s32[8,512,4]{2,1,0:T(8,128)}, /*index...) while((s32[]{:T(128)}, f32[8,3,512]{2,1,0:T(4,128)S(1)}, ...), condition=%wide.region_4.5_spmd, body=%wide.region_1.4_spmd.sunk | while | flops 6574084 | bytes 65403084 | solution.py:111
  54.9 19.5 %gather_fusion = f32[2048,6,128]{2,1,0:T(8,128)} fusion(f32[6,2244,128]{2,0,1:T(8,128)} %get-tuple-element.240, s32[2048]{0:T(1024)S(1)} %broadcast_clamp_fusion.3), kind=kCustom, calls=%fused_computation.clone.1 | custom fusion | bytes 12591104 | tf_op jit(solution)/shard_map/while/body/eval_jaxpr/jit(_take)/gather | solution.py:108
  74.5 11.2 %select_bitcast_fusion.2 = f32[6,2048,128]{2,0,1:T(8,128)S(1)} fusion(f32[2048,6,128]{2,1,0:T(8,128)} %gather_fusion, pred[2048]{0:T(1024)(128)(4,1)S(1)} %compare_and_fusion.2), kind=kLoop, calls=%fused_computation.3.clone.1 | loop fusion | flops 1572864 | bytes 12584960 | tf_op jit(solution)/shard_map/while/body/eval_jaxpr/jit(_take)/select_n | solution.py:108
  85.8 3.3 copy-done
  89.1 2.2 fusion.29
  97.9 5.8 fusion.30
  106.4 19.5 %gather_fusion = f32[2048,6,128]{2,1,0:T(8,128)} fusion(f32[6,2244,128]{2,0,1:T(8,128)} %get-tuple-element.240, s32[2048]{0:T(1024)S(1)} %broadcast_clamp_fusion.3), kind=kCustom, calls=%fused_computation.clone.1 | custom fusion | bytes 12591104 | tf_op jit(solution)/shard_map/while/body/eval_jaxpr/jit(_take)/gather | solution.py:108
  126.0 11.2 %select_bitcast_fusion.2 = f32[6,2048,128]{2,0,1:T(8,128)S(1)} fusion(f32[2048,6,128]{2,1,0:T(8,128)} %gather_fusion, pred[2048]{0:T(1024)(128)(4,1)S(1)} %compare_and_fusion.2), kind=kLoop, calls=%fused_computation.3.clone.1 | loop fusion | flops 1572864 | bytes 12584960 | tf_op jit(solution)/shard_map/while/body/eval_jaxpr/jit(_take)/select_n | solution.py:108
  137.3 3.3 copy-done
  140.6 2.2 fusion.29
  149.4 5.8 fusion.30
  157.9 19.5 %gather_fusion = f32[2048,6,128]{2,1,0:T(8,128)} fusion(f32[6,2244,128]{2,0,1:T(8,128)} %get-tuple-element.240, s32[2048]{0:T(1024)S(1)} %broadcast_clamp_fusion.3), kind=kCustom, calls=%fused_computation.clone.1 | custom fusion | bytes 12591104 | tf_op jit(solution)/shard_map/while/body/eval_jaxpr/jit(_take)/gather | solution.py:108
  177.6 11.2 %select_bitcast_fusion.2 = f32[6,2048,128]{2,0,1:T(8,128)S(1)} fusion(f32[2048,6,128]{2,1,0:T(8,128)} %gather_fusion, pred[2048]{0:T(1024)(128)(4,1)S(1)} %compare_and_fusion.2), kind=kLoop, calls=%fused_computation.3.clone.1 | loop fusion | flops 1572864 | bytes 12584960 | tf_op jit(solution)/shard_map/while/body/eval_jaxpr/jit(_take)/select_n | solution.py:108
  188.8 3.3 copy-done
  192.1 2.2 fusion.29
  200.9 5.8 fusion.30
  209.4 19.5 %gather_fusion = f32[2048,6,128]{2,1,0:T(8,128)} fusion(f32[6,2244,128]{2,0,1:T(8,128)} %get-tuple-element.240, s32[2048]{0:T(1024)S(1)} %broadcast_clamp_fusion.3), kind=kCustom, calls=%fused_computation.clone.1 | custom fusion | bytes 12591104 | tf_op jit(solution)/shard_map/while/body/eval_jaxpr/jit(_take)/gather | solution.py:108
  229.1 11.2 %select_bitcast_fusion.2 = f32[6,2048,128]{2,0,1:T(8,128)S(1)} fusion(f32[2048,6,128]{2,1,0:T(8,128)} %gather_fusion, pred[2048]{0:T(1024)(128)(4,1)S(1)} %compare_and_fusion.2), kind=kLoop, calls=%fused_computation.3.clone.1 | loop fusion | flops 1572864 | bytes 12584960 | tf_op jit(solution)/shard_map/while/body/eval_jaxpr/jit(_take)/select_n | solution.py:108
  240.3 3.3 copy-done
  243.6 2.2 fusion.29
  252.4 5.8 fusion.30
  260.9 19.5 %gather_fusion = f32[2048,6,128]{2,1,0:T(8,128)} fusion(f32[6,2244,128]{2,0,1:T(8,128)} %get-tuple-element.240, s32[2048]{0:T(1024)S(1)} %broadcast_clamp_fusion.3), kind=kCustom, calls=%fused_computation.clone.1 | custom fusion | bytes 12591104 | tf_op jit(solution)/shard_map/while/body/eval_jaxpr/jit(_take)/gather | solution.py:108
  280.6 11.2 %select_bitcast_fusion.2 = f32[6,2048,128]{2,0,1:T(8,128)S(1)} fusion(f32[2048,6,128]{2,1,0:T(8,128)} %gather_fusion, pred[2048]{0:T(1024)(128)(4,1)S(1)} %compare_and_fusion.2), kind=kLoop, calls=%fused_computation.3.clone.1 | loop fusion | flops 1572864 | bytes 12584960 | tf_op jit(solution)/shard_map/while/body/eval_jaxpr/jit(_take)/select_n | solution.py:108
  291.8 3.3 copy-done
  295.1 2.2 fusion.29
  304.0 5.8 fusion.30
  312.4 19.5 %gather_fusion = f32[2048,6,128]{2,1,0:T(8,128)} fusion(f32[6,2244,128]{2,0,1:T(8,128)} %get-tuple-element.240, s32[2048]{0:T(1024)S(1)} %broadcast_clamp_fusion.3), kind=kCustom, calls=%fused_computation.clone.1 | custom fusion | bytes 12591104 | tf_op jit(solution)/shard_map/while/body/eval_jaxpr/jit(_take)/gather | solution.py:108
  332.1 11.2 %select_bitcast_fusion.2 = f32[6,2048,128]{2,0,1:T(8,128)S(1)} fusion(f32[2048,6,128]{2,1,0:T(8,128)} %gather_fusion, pred[2048]{0:T(1024)(128)(4,1)S(1)} %compare_and_fusion.2), kind=kLoop, calls=%fused_computation.3.clone.1 | loop fusion | flops 1572864 | bytes 12584960 | tf_op jit(solution)/shard_map/while/body/eval_jaxpr/jit(_take)/select_n | solution.py:108
  343.3 3.3 copy-done
  346.6 2.2 fusion.29
  355.5 5.8 fusion.30
  363.9 19.5 %gather_fusion = f32[2048,6,128]{2,1,0:T(8,128)} fusion(f32[6,2244,128]{2,0,1:T(8,128)} %get-tuple-element.240, s32[2048]{0:T(1024)S(1)} %broadcast_clamp_fusion.3), kind=kCustom, calls=%fused_computation.clone.1 | custom fusion | bytes 12591104 | tf_op jit(solution)/shard_map/while/body/eval_jaxpr/jit(_take)/gather | solution.py:108
  383.6 11.2 %select_bitcast_fusion.2 = f32[6,2048,128]{2,0,1:T(8,128)S(1)} fusion(f32[2048,6,128]{2,1,0:T(8,128)} %gather_fusion, pred[2048]{0:T(1024)(128)(4,1)S(1)} %compare_and_fusion.2), kind=kLoop, calls=%fused_computation.3.clone.1 | loop fusion | flops 1572864 | bytes 12584960 | tf_op jit(solution)/shard_map/while/body/eval_jaxpr/jit(_take)/select_n | solution.py:108
  394.8 3.3 copy-done
  398.1 2.2 fusion.29
  407.0 5.8 fusion.30
  415.4 19.5 %gather_fusion = f32[2048,6,128]{2,1,0:T(8,128)} fusion(f32[6,2244,128]{2,0,1:T(8,128)} %get-tuple-element.240, s32[2048]{0:T(1024)S(1)} %broadcast_clamp_fusion.3), kind=kCustom, calls=%fused_computation.clone.1 | custom fusion | bytes 12591104 | tf_op jit(solution)/shard_map/while/body/eval_jaxpr/jit(_take)/gather | solution.py:108
  435.1 11.2 %select_bitcast_fusion.2 = f32[6,2048,128]{2,0,1:T(8,128)S(1)} fusion(f32[2048,6,128]{2,1,0:T(8,128)} %gather_fusion, pred[2048]{0:T(1024)(128)(4,1)S(1)} %compare_and_fusion.2), kind=kLoop, calls=%fused_computation.3.clone.1 | loop fusion | flops 1572864 | bytes 12584960 | tf_op jit(solution)/shard_map/while/body/eval_jaxpr/jit(_take)/select_n | solution.py:108
  446.3 3.3 copy-done
  449.6 2.2 fusion.29
  458.5 5.8 fusion.30
  466.4 97.2 %scatter_custom_fusion = f32[3,262144]{0,1:T(8,128)} fusion(s32[4096]{0:T(1024)} %get-tuple-element.80, f32[]{:T(128)} %constant.118.clone.1, f32[4096,3]{1,0:T(8,128)S(1)} %copy.81, s32[4096]{0:T(1024)S(1)} %broadcast_clamp_fusion.1), kind=kCustom, calls=%fused_computation.19 | custom fusion | flops 12288 | bytes 3146240 | tf_op jit(solution)/shard_map/scatter-add | solution.py:119
  563.7 69.1 %copy.82 = f32[3,128,8,256]{3,0,2,1:T(4,128)} copy(f32[3,128,8,256]{0,3,2,1:T(8,128)} %bitcast.26) | data formatting | bytes 6291456 | tf_op jit(solution)/shard_map/reshape;reshape | solution.py:31
  632.8 2.7 fusion.25
  638.7 36.6 %all-reduce.44.cloned.1.call-done = f32[128,3,1,256]{3,1,2,0:T(4,128)} async-done(((f32[128,3,1,256]{3,1,2,0:T(4,128)}), f32[128,3,1,256]{3,1,2,0:T(4,128)}) %all-reduce.44.cloned.1.call-update) | async-done | bytes 393232
  680.0 24.1 %all-reduce.56.cloned.1.call-done = (f32[128,3,1,256]{3,1,2,0:T(4,128)}, f32[64,3,1,256]{3,1,2,0:T(4,128)}) async-done(((f32[128,3,1,256]{3,1,2,0:T(4,128)}, f32[64,3,1,256]{3,1,2,0:T(4,128)}), (f32[128,3,1,256]{3,1,2,0:T(4,128)}, f32[64,3,1,256]{3,1,2,0:T(4,128)})) %all-reduce.56.cloned.1.call-update) | async-done | bytes 589840
  713.2 40.5 %all-reduce.52.cloned.1.call-done = (f32[64,3,1,256]{3,1,2,0:T(4,128)}, f32[128,3,1,256]{3,1,2,0:T(4,128)}, f32[32,3,1,256]{3,1,2,0:T(4,128)}) async-done(((f32[64,3,1,256]{3,1,2,0:T(4,128)}, f32[128,3,1,256]{3,1,2,0:T(4,128)}, f32[32,3,1,256]{3,1,2,0:T(4,128)}), (f32[64,3,1,256]{3,1,2,0:T(4,128)}, f32[128,3,1,256]{3,1,2,0:T(4,128)}, f32[32,3,1,256]{3,1,2,0:T(4,128)})) %all-reduce.52.cloned.1.call-update) | async-done | bytes 688144
  758.3 54.7 %all-reduce.46.cloned.1.call-done = (f32[32,3,1,256]{3,1,2,0:T(4,128)}, f32[64,3,1,256]{3,1,2,0:T(4,128)}, f32[128,3,4,256]{3,2,1,0:T(4,128)}) async-done(((f32[32,3,1,256]{3,1,2,0:T(4,128)}, f32[64,3,1,256]{3,1,2,0:T(4,128)}, f32[128,3,4,256]{3,2,1,0:T(4,128)}), (f32[32,3,1,256]{3,1,2,0:T(4,128)}, f32[64,3,1,256]{3,1,2,0:T(4,128)}, f32[128,3,4,256]{3,2,1,0:T(4,128)})) %all-reduce.46.cloned.1.call-update) | async-done | bytes 1867792
  824.7 33.7 %all-reduce.50.cloned.1.call-done = (f32[128,3,1,256]{3,1,2,0:T(4,128)}, f32[32,3,4,256]{3,2,1,0:T(4,128)}) async-done(((f32[128,3,1,256]{3,1,2,0:T(4,128)}, f32[32,3,4,256]{3,2,1,0:T(4,128)}), (f32[128,3,1,256]{3,1,2,0:T(4,128)}, f32[32,3,4,256]{3,2,1,0:T(4,128)})) %all-reduce.50.cloned.1.call-update) | async-done | bytes 786448
  863.1 30.6 %all-reduce.58.cloned.1.call-done = (f32[32,3,1,256]{3,1,2,0:T(4,128)}, f32[8,3,4,256]{3,2,1,0:T(4,128)}) async-done(((f32[32,3,1,256]{3,1,2,0:T(4,128)}, f32[8,3,4,256]{3,2,1,0:T(4,128)}), (f32[32,3,1,256]{3,1,2,0:T(4,128)}, f32[8,3,4,256]{3,2,1,0:T(4,128)})) %all-reduce.58.cloned.1.call-update) | async-done | bytes 196624
  898.1 24.2 %all-reduce.54.cloned.1.call-done = (f32[16,3,1,256]{3,1,2,0:T(4,128)}, f32[4,3,4,256]{3,2,1,0:T(4,128)}) async-done(((f32[16,3,1,256]{3,1,2,0:T(4,128)}, f32[4,3,4,256]{3,2,1,0:T(4,128)}), (f32[16,3,1,256]{3,1,2,0:T(4,128)}, f32[4,3,4,256]{3,2,1,0:T(4,128)})) %all-reduce.54.cloned.1.call-update) | async-done | bytes 98320
  923.8 10.0 all-reduce.29
  933.8 14.1 %all-reduce.25 = (f32[4,3,1,256]{3,1,2,0:T(4,128)S(1)}, f32[16,3,1,256]{3,1,2,0:T(4,128)S(1)}) all-reduce(f32[4,3,1,256]{3,1,2,0:T(4,128)S(1)} %constant_dynamic-slice_fusion.26, f32[16,3,1,256]{3,1,2,0:T(4,128)S(1)} %constant_dynamic-slice_fusion.22), channel_id=6, replica_groups=mesh['bx_0'=4,'bx_1'=2,'bx_2'=2,'by_0'=2,'by_1'=4] {'by_1'}, use_global_device_ids=true, to_apply=%region_10.11.clone | all-reduce | flops 15360 | bytes 122880
  949.8 40.9 %all-reduce.48.cloned.1.call-done = (f32[4,3,1,256]{3,1,2,0:T(4,128)}, f32[8,3,1,256]{3,1,2,0:T(4,128)}, f32[16,3,1,256]{3,1,2,0:T(4,128)}) async-done(((f32[4,3,1,256]{3,1,2,0:T(4,128)}, f32[8,3,1,256]{3,1,2,0:T(4,128)}, f32[16,3,1,256]{3,1,2,0:T(4,128)}), (f32[4,3,1,256]{3,1,2,0:T(4,128)}, f32[8,3,1,256]{3,1,2,0:T(4,128)}, f32[16,3,1,256]{3,1,2,0:T(4,128)})) %all-reduce.48.cloned.1.call-update) | async-done | bytes 86032
  992.2 6.3 all-reduce.33
  998.5 7.1 all-reduce.19
  (274 shorter events, 127.4 us)
Async XLA Ops:
  6.5 668.8 %all-reduce.44.cloned.1.call-start = ((), (), s32[]{:S(2)}) async-start(), calls=%async_computation | async-start | bytes 1048576
  11.4 1.6 copy-start.1
  11.4 5.3 copy-start.6
  11.4 5.6 copy-start.4
  13.8 19.5 %collective-permute-start = (f32[6,1,32,128]{3,2,1,0:T(8,128)}, f32[6,1,32,128]{3,2,1,0:T(8,128)S(1)}, u32[]{:S(2)}, u32[]{:S(2)}) collective-permute-start(f32[6,1,32,128]{3,2,1,0:T(8,128)} %get-tuple-element.134), channel_id=1, source_target_pairs={{0,8},{8,16},{16,24},{24,32},{32,40},{40,48},{48,56},{56,64},{64,7... | collective-permute-start | bytes 294920 | tf_op jit(solution)/shard_map/ppermute | solution.py:23
  16.8 16.5 %collective-permute-start.1 = (f32[6,1,32,128]{3,2,1,0:T(8,128)}, f32[6,1,32,128]{3,2,1,0:T(8,128)S(1)}, u32[]{:S(2)}, u32[]{:S(2)}) collective-permute-start(f32[6,1,32,128]{3,2,1,0:T(8,128)} %get-tuple-element.135), channel_id=1, source_target_pairs={{8,0},{16,8},{24,16},{32,24},{40,32},{48,40},{56,48},{64,56},{72,6... | collective-permute-start | bytes 294920 | tf_op jit(solution)/shard_map/ppermute | solution.py:24
  21.5 6.0 copy-start.5
  33.3 11.5 %copy-start.2 = (f32[3,64,32,128]{3,2,1,0:T(8,128)S(1)}, f32[3,64,32,128]{3,2,1,0:T(8,128)}, u32[]{:S(2)}) copy-start(f32[3,64,32,128]{3,2,1,0:T(8,128)} %copy-done.1) | copy-start | bytes 9437188
  35.2 9.1 collective-permute-start.2
  36.5 8.0 collective-permute-start.3
  47.9 5.8 copy-start.3
  85.7 3.3 copy-start
  137.3 3.3 copy-start
  188.8 3.3 copy-start
  240.3 3.3 copy-start
  291.8 3.3 copy-start
  343.3 3.3 copy-start
  394.8 3.3 copy-start
  446.3 3.3 copy-start
  632.8 3.8 copy-start.12
  632.8 44.3 %copy-start.11 = (u32[128]{0:T(128)S(1)}, u32[128]{0:T(128)}, u32[]{:S(2)}) copy-start(u32[128]{0:T(128)} %constant.148) | copy-start | bytes 1540
  635.5 71.9 %copy-start.10 = (u32[128]{0:T(128)S(1)}, u32[128]{0:T(128)}, u32[]{:S(2)}) copy-start(u32[128]{0:T(128)} %constant.152) | copy-start | bytes 1540
  636.5 67.6 %all-reduce.56.cloned.1.call-start = ((), (), s32[]{:S(2)}) async-start(), calls=%async_computation.6 | async-start | bytes 1572864
  677.1 76.6 %all-reduce.52.cloned.1.call-start = ((), (), s32[]{:S(2)}) async-start(), calls=%async_computation.4 | async-start | bytes 1835008
  707.4 105.6 %all-reduce.46.cloned.1.call-start = ((), (), s32[]{:S(2)}) async-start(), calls=%async_computation.1 | async-start | bytes 3932160
  711.5 45.6 %copy-start.9 = (u32[128]{0:T(128)S(1)}, u32[128]{0:T(128)}, u32[]{:S(2)}) copy-start(u32[128]{0:T(128)} %constant.156) | copy-start | bytes 1540
  711.5 103.4 %copy-start.8 = (u32[128]{0:T(128)S(1)}, u32[128]{0:T(128)}, u32[]{:S(2)}) copy-start(u32[128]{0:T(128)} %constant.140) | copy-start | bytes 1540
  753.7 107.9 %copy-start.7 = (f32[32,3,1,256]{3,1,2,0:T(4,128)S(1)}, f32[32,3,1,256]{3,1,2,0:T(4,128)}, u32[]{:S(2)}) copy-start(f32[32,3,1,256]{3,1,2,0:T(4,128)} %get-tuple-element.112) | copy-start | bytes 294916
  757.0 101.4 %all-reduce.50.cloned.1.call-start = ((), (), s32[]{:S(2)}) async-start(), calls=%async_computation.3 | async-start | bytes 1835008
  814.8 79.0 %all-reduce.58.cloned.1.call-start = ((), (), s32[]{:S(2)}) async-start(), calls=%async_computation.7 | async-start | bytes 458752
  861.6 60.7 %all-reduce.54.cloned.1.call-start = ((), (), s32[]{:S(2)}) async-start(), calls=%async_computation.5 | async-start | bytes 229376
  896.7 94.1 %all-reduce.48.cloned.1.call-start = ((), (), s32[]{:S(2)}) async-start(), calls=%async_computation.2 | async-start | bytes 229376
Sparse Core Ops, SparseCore 0:
  636.6 38.6 all-reduce.43
  677.8 26.1 all-reduce.55
  707.5 46.1 all-reduce.51
  757.2 55.7 all-reduce.45
  815.3 43.1 all-reduce.49
  861.7 32.0 all-reduce.57
  896.8 25.4 all-reduce.53
  949.2 41.4 all-reduce.47
where the time goes:
time: 1030 us; the launch traced here: 1020 us
  local copies, waits for them, and re-layouts  373 us (36%)
  waiting for transfers between devices  288 us (28%)
  other arithmetic  279 us (27%)
  blocking collectives  37.5 us (4%)
  between operations  27.4 us (3%)
    unnamed x16, waiting for transfers between devices  285 us
    gather x8, local copies, waits for them, and re-layouts, one_group(): jnp.take(table, idb.reshape(-1), axis=1).reshape(6, group, listed, slots)  156 us
    scatter-add x3, other arithmetic, per_device(): jnp.zeros((3, tiles * TILE_PIX), jnp.float32).at[:, target].add(radiance)  103 us
    select_n x16, other arithmetic, one_group(): jnp.take(table, idb.reshape(-1), axis=1).reshape(6, group, listed, slots)  89.7 us
    another operation x1, local copies, waits for them, and re-layouts, cut_along(): return jnp.moveaxis(x.reshape(*before, peers, -1, *after), dim, 0)  69.1 us
    reduce_sum x16, other arithmetic, kernel_sum(): sums = jnp.sum(weight[None] * blocks[3:6], axis=(2, 3))  51.5 us
    unnamed x4, blocking collectives  37.5 us
    unnamed x50, local copies, waits for them, and re-layouts  28.1 us
  transfers between devices with their start and end apart: 12, of which 9 were waited for; matrix products, arithmetic and copies ran while one was open for 3% of the time, Pallas kernels for 0%

commit v1 on v0

v1 whole, which is shorter than its diff:
```python
import jax
import jax.numpy as jnp
from jax import lax
from jax.experimental import pallas as pl
from jax.experimental.pallas import tpu as pltpu
from jax.sharding import PartitionSpec as P

MESH = pl.DeviceIdType.MESH
F32, BF16, I32 = jnp.float32, jnp.bfloat16, jnp.int32
CX, CY, SLOTS, G = 64, 32, 128, 4096
NXC, NYC = 1024, 256
PITCH = 2 * (CY + 2)
PAD = 8
NR = 4432
FAR = 1.0e9
OWNERS = 128
TILES = G // 128


def iota(shape, dim):
    return lax.broadcasted_iota(I32, shape, dim)


def split(x):
    high = x.astype(BF16).astype(F32)
    return high, x - high


def build_table(ph, cnt, xf, yf, table, cb):
    eye = iota((CY, CY), 0) == iota((CY, CY), 1)
    spread = jnp.where(eye[None], cnt[...][:, None, :], 0.0).reshape(CX * CY, CY)
    cb[...] = jnp.dot(spread.astype(BF16), jnp.ones((CY, SLOTS), BF16), preferred_element_type=F32)
    slot = iota((8, SLOTS), 1).astype(F32)
    sub = iota((8, SLOTS), 0).astype(F32)

    def change(c, v, x, y):
        if c == 0:
            return 2.0 * (v + x)
        if c == 1:
            return 2.0 * (v + y)
        return 2.0 * v if c == 2 else v

    def put(c, x, n, v, first, last):
        base = c * NR + PAD + x * PITCH + 2 * (1 + 8 * n)
        if not last:
            table[pl.ds(base, 8, stride=2), :] = v
        if not first:
            table[pl.ds(base - PITCH + 1, 8, stride=2), :] = v

    def one_x(x, carry):
        xs = (x + 1).astype(F32)
        for n in range(CY // 8):
            live = slot < cb[pl.ds(x * CY + 8 * n, 8), :]
            for c in range(6):
                v = change(c, ph[c, x, 8 * n : 8 * n + 8, :], xs, sub + (1.0 + 8 * n))
                if c == 0:
                    v = jnp.where(live, v, FAR)
                put(c, x + 1, n, v, False, False)
        return carry

    lax.fori_loop(0, CX, one_x, 0)
    for side, x in ((0, 0), (1, CX + 1)):
        for n in range(CY // 8):
            for c in range(6):
                v = change(c, xf[side, c, 8 * n : 8 * n + 8, :], float(x), sub + (1.0 + 8 * n))
                put(c, x, n, v, side == 0, side == 1)
    for side, y in ((0, 0), (1, CY + 1)):
        for c in range(6):
            for shift in (0, 1):
                for n in range(9):
                    rows = 8 if n < 8 else 1
                    xs = sub[:rows] + float(8 * n + shift)
                    v = change(c, yf[side, c, pl.ds(8 * n + shift, rows), :], xs, float(y))
                    base = c * NR + PAD + 8 * n * PITCH + 2 * y + shift
                    table[pl.ds(base, rows, stride=PITCH), :] = v


def sum_photons(idx, off, table, prod, sums):
    half = iota((8, SLOTS), 0) < 4

    def chunk(i, carry):
        for u in range(2):
            g0 = i * 16 + 8 * u
            for pair in range(4):
                p, q = g0 + 2 * pair, g0 + 2 * pair + 1
                rp, rq = idx[p], idx[q] - 4
                v = []
                for c in range(6):
                    a = table[pl.ds(rp + c * NR, 8), :]
                    b = table[pl.ds(rq + c * NR, 8), :]
                    if c < 3:
                        a, b = a - off[c * G + p], b - off[c * G + q]
                    v.append(jnp.where(half, a, b))
                w = jnp.maximum(1.0 - (v[0] * v[0] + v[1] * v[1] + v[2] * v[2]), 0.0)
                for c in range(3):
                    prod[c, u, 8 * pair : 8 * pair + 8, :] = w * v[3 + c]
            for c in range(3):
                s = [prod[c, u, pl.ds(k, 8, stride=4), :] for k in range(4)]
                sums[c, pl.ds(pl.multiple_of(g0, 8), 8), :] = (s[0] + s[1]) + (s[2] + s[3])
        return carry

    lax.fori_loop(0, G // 16, chunk, 0)


def pack(alb, pix, ts, sums, out, lhs, rt, carry):
    t = ts[...]
    lookup = jnp.concatenate([t >> 3, t & 7], axis=0).astype(F32).astype(BF16)
    rows = iota((128, 128), 0)
    cols = iota((128, 128), 1)
    eye = rows == cols
    before = jnp.where(rows < cols, 1.0, 0.0).astype(BF16)
    ones = jnp.ones((128, 128), BF16)
    before = jnp.concatenate([before, ones], axis=1)
    eight = iota((8, 128), 0)
    carry[...] = jnp.zeros((128, 128), F32)

    def tile(j, unused):
        at = pl.ds(pl.multiple_of(j * 128, 128), 128)
        pixel = pix[pl.ds(j, 1), :]
        image = pixel >> 8
        hot = (rows == (image & 127)).astype(F32).astype(BF16)
        found = jnp.dot(lookup, hot, preferred_element_type=F32)
        pick = eight == (image >> 7)
        owner = jnp.sum(jnp.where(pick, found[:8], 0.0), axis=0, keepdims=True)
        inner = jnp.sum(jnp.where(pick, found[8:], 0.0), axis=0, keepdims=True)
        mine = rows == owner.astype(I32)
        counts = jnp.dot(mine.astype(F32).astype(BF16), before, preferred_element_type=F32)
        rank = jnp.sum(jnp.where(mine, counts[:, :128] + carry[...], 0.0), axis=0, keepdims=True)
        carry[...] += counts[:, 128:]
        rt[:, at] = (rows == rank.astype(I32)).astype(F32).astype(BF16)
        local = inner * 256.0 + (pixel & 255).astype(F32)
        high = jnp.floor(local * (1.0 / 128.0))
        kinds = []
        for c in range(3):
            a, b = split(sums[c, at, :])
            total = jnp.dot(a.astype(BF16), ones, preferred_element_type=F32)
            total += jnp.dot(b.astype(BF16), ones, preferred_element_type=F32)
            row = jnp.sum(jnp.where(eye, total, 0.0), axis=0, keepdims=True)
            kinds.extend(split(row * alb[c, pl.ds(j, 1), :]))
        kinds.extend([high, local - 128.0 * high])
        for k, row in enumerate(kinds):
            lhs[128 * k : 128 * k + 128, at] = jnp.where(mine, row, 0.0).astype(BF16)
        return unused

    lax.fori_loop(0, TILES, tile, 0)
    for c in range(4):
        part = lax.dot_general(
            lhs[256 * c : 256 * c + 256, :], rt[...], (((1,), (1,)), ((), ())), preferred_element_type=F32
        )
        a, b = part[:128], part[128:]
        out[pl.ds(c, 128, stride=4), :] = a + b if c < 3 else 128.0 * a + b


def radiance_kernel(idx, off, ph, cnt, xf, yf, alb, pix, ts, out, table, cb, prod, sums, lhs, rt, carry):
    build_table(ph, cnt, xf, yf, table, cb)
    sum_photons(idx, off, table, prod, sums)
    pack(alb, pix, ts, sums, out, lhs, rt, carry)


def radiance_call(idx, off, ph, cnt, xf, yf, alb, pix, ts):
    smem = pl.BlockSpec(memory_space=pltpu.SMEM)
    vmem = pl.BlockSpec(memory_space=pltpu.VMEM)
    return pl.pallas_call(
        radiance_kernel,
        out_shape=jax.ShapeDtypeStruct((4 * OWNERS, 128), F32),
        in_specs=[smem] * 2 + [vmem] * 7,
        out_specs=vmem,
        scratch_shapes=[
            pltpu.VMEM((6 * NR, SLOTS), F32),
            pltpu.VMEM((CX * CY, SLOTS), F32),
            pltpu.VMEM((3, 2, 32, SLOTS), F32),
            pltpu.VMEM((3, G, SLOTS), F32),
            pltpu.VMEM((8 * 128, G), BF16),
            pltpu.VMEM((128, G), BF16),
            pltpu.VMEM((128, 128), F32),
        ],
        compiler_params=pltpu.CompilerParams(vmem_limit_bytes=60 << 20),
        name="radiance",
    )(idx, off, ph, cnt, xf, yf, alb, pix, ts)


def film_kernel(got, film, lhs, rt):
    rows = iota((128, 128), 0)
    sixteen = iota((16, 128), 0)

    def source(s, unused):
        at = pl.ds(pl.multiple_of(s * 128, 128), 128)
        pixel = got[pl.ds(4 * s + 3, 1), :].astype(I32)
        rt[:, at] = (rows == (pixel & 127)).astype(F32).astype(BF16)
        spot = sixteen == ((pixel >> 7) & 1) * 8 + (pixel >> 8)
        for c in range(3):
            for k, part in enumerate(split(got[pl.ds(4 * s + c, 1), :])):
                at_row = 16 * (2 * c + k)
                lhs[at_row : at_row + 16, at] = jnp.where(spot, part, 0.0).astype(BF16)
        return unused

    lax.fori_loop(0, OWNERS, source, 0)
    total = lax.dot_general(lhs[...], rt[...], (((1,), (1,)), ((), ())), preferred_element_type=F32)
    for c in range(3):
        both = total[32 * c : 32 * c + 16] + total[32 * c + 16 : 32 * c + 32]
        film[c, :, 0:128] = both[:8]
        film[c, :, 128:256] = both[8:]


def film_call(got):
    vmem = pl.BlockSpec(memory_space=pltpu.VMEM)
    return pl.pallas_call(
        film_kernel,
        out_shape=jax.ShapeDtypeStruct((3, 8, 256), F32),
        in_specs=[vmem],
        out_specs=vmem,
        scratch_shapes=[pltpu.VMEM((96, OWNERS * 128), BF16), pltpu.VMEM((128, OWNERS * 128), BF16)],
        compiler_params=pltpu.CompilerParams(vmem_limit_bytes=60 << 20),
        name="film",
    )(got)


def exchange_kernel(send, got, send_sem, recv_sem, own_sem):
    nx, ny = lax.axis_size("bx"), lax.axis_size("by")
    n = nx * ny
    me = lax.axis_index("bx") * ny + lax.axis_index("by")
    barrier = pltpu.get_barrier_semaphore()

    def greet(k, unused):
        peer = lax.rem(me + k, n)
        pl.semaphore_signal(barrier, inc=1, device_id=(peer // ny, lax.rem(peer, ny)), device_id_type=MESH)
        return unused

    lax.fori_loop(1, n, greet, 0)
    own = pltpu.make_async_copy(send.at[pl.ds(me, 1)], got.at[pl.ds(me, 1)], own_sem)
    own.start()
    pl.semaphore_wait(barrier, n - 1)

    def ship(k, unused):
        peer = lax.rem(me + k, n)
        pltpu.make_async_remote_copy(
            src_ref=send.at[pl.ds(peer, 1)],
            dst_ref=got.at[pl.ds(me, 1)],
            send_sem=send_sem,
            recv_sem=recv_sem,
            device_id=(peer // ny, lax.rem(peer, ny)),
            device_id_type=MESH,
        ).start()
        return unused

    lax.fori_loop(1, n, ship, 0)
    own.wait()
    for sem in (send_sem, recv_sem):
        pltpu.make_async_copy(send.at[pl.ds(0, n - 1)], got.at[pl.ds(0, n - 1)], sem).wait()


def exchange_call(blocks):
    vmem = pl.BlockSpec(memory_space=pltpu.VMEM)
    return pl.pallas_call(
        exchange_kernel,
        out_shape=jax.ShapeDtypeStruct(blocks.shape, F32),
        in_specs=[vmem],
        out_specs=vmem,
        scratch_shapes=[pltpu.SemaphoreType.DMA, pltpu.SemaphoreType.DMA, pltpu.SemaphoreType.DMA],
        compiler_params=pltpu.CompilerParams(collective_id=1, has_side_effects=True),
        name="exchange",
    )(blocks)


def ring(n):
    up = [(i, (i + 1) % n) for i in range(n)]
    return up, [(j, i) for i, j in up]


def per_device(photon_data, block_counts, gather_offsets, gather_blocks, albedo, gather_pixels, tile_slot):
    ix, iy = lax.axis_index("bx"), lax.axis_index("by")
    nx, ny = lax.axis_size("bx"), lax.axis_size("by")
    slot = iota((SLOTS,), 0)

    def masked(face, counts):
        x = jnp.where(slot < counts[..., None], face[0], FAR)
        return jnp.concatenate([x[None], face[1:]], axis=0)

    up, down = ring(nx)
    xlo = lax.ppermute(masked(photon_data[:, CX - 1], block_counts[CX - 1]), "bx", up)
    xhi = lax.ppermute(masked(photon_data[:, 0], block_counts[0]), "bx", down)
    up, down = ring(ny)

    def yface(y):
        own = masked(photon_data[:, :, y], block_counts[:, y])
        return jnp.concatenate([xlo[:, y][:, None], own, xhi[:, y][:, None]], axis=1)

    ylo = lax.ppermute(yface(CY - 1), "by", up)
    yhi = lax.ppermute(yface(0), "by", down)
    lx = (gather_blocks // NYC - ix * CX + 1) % NXC
    ly = (gather_blocks % NYC - iy * CY + 1) % NYC
    index = PAD + jnp.min(lx, axis=0) * PITCH + 2 * jnp.min(ly, axis=0)
    off = 2.0 * jnp.concatenate(
        [lx[0].astype(F32) + gather_offsets[0], ly[0].astype(F32) + gather_offsets[1], gather_offsets[2]]
    )
    blocks = radiance_call(
        index,
        off,
        photon_data,
        block_counts.astype(F32),
        jnp.stack([xlo, xhi]),
        jnp.stack([ylo, yhi]),
        albedo.reshape(3, TILES, 128),
        gather_pixels.reshape(TILES, 128),
        tile_slot.reshape(8, 128),
    )
    got = exchange_call(blocks.reshape(OWNERS, 4, 128))
    return film_call(got.reshape(4 * OWNERS, 128))


def solution(mesh):
    in_specs = (
        P(None, "bx", "by", None),
        P("bx", "by"),
        P(None, ("bx", "by")),
        P(None, ("bx", "by")),
        P(None, ("bx", "by")),
        P(("bx", "by")),
        P(),
    )
    out_specs = P(None, ("bx", "by"), None)
    return jax.shard_map(per_device, mesh=mesh, in_specs=in_specs, out_specs=out_specs, check_vma=False)
```

time: 1030 us -> 85.3 us (0.08); the launches traced: 1020 us -> 84.7 us
  local copies, waits for them, and re-layouts: 373 us -> 7.85 us
  waiting for transfers between devices: 288 us -> 0.01 us
  other arithmetic: 279 us -> 6.66 us
  Pallas kernels: 0 us -> 61 us
  blocking collectives: 37.5 us -> 0 us
  between operations: 27.4 us -> 0.09 us
    unnamed x16 -> x0, waiting for transfers between devices: 285 us -> none
    gather x8 -> x0, local copies, waits for them, and re-layouts: 156 us -> none  [one_group(): jnp.take(table, idb.reshape(-1), axis=1).reshape(6, group, listed, slots)]
    scatter-add x3 -> x0, other arithmetic: 103 us -> none  [per_device(): jnp.zeros((3, tiles * TILE_PIX), jnp.float32).at[:, target].add(radiance)]
    select_n x18 -> x3, other arithmetic: 90.4 us -> 0.96 us  [masked(): x = jnp.where(slot < counts[..., None], face[0], FAR)]
    another operation x1 -> x0, local copies, waits for them, and re-layouts: 69.1 us -> none  [cut_along(): return jnp.moveaxis(x.reshape(*before, peers, -1, *after), dim, 0)]
    pallas_call x0 -> x3, Pallas kernels: none -> 61 us  [the longest x1 34.7 us: radiance_call(): pl.pallas_call(radiance_kernel, out_shape=jax.ShapeDtypeStruct((4 * OWNER...]
    reduce_sum x17 -> x0, other arithmetic: 55.3 us -> none  [the longest x16 51.5 us: kernel_sum(): sums = jnp.sum(weight[None] * blocks[3:6], axis=(2, 3))]
    unnamed x4 -> x0, blocking collectives: 37.5 us -> none
  transfers between devices with their start and end apart: 12 -> 4, of which waited for: 9 -> 0; matrix products, arithmetic and copies ran while one was open for 3% -> 13% of each run, Pallas kernels for 0% -> 0%
where the time goes in v1:
time: 85.3 us; the launch traced here: 84.7 us
  Pallas kernels  61 us (72%)
  starting transfers between devices  9.06 us (11%)
  local copies, waits for them, and re-layouts  7.85 us (9%)
  other arithmetic  6.66 us (8%)
    pallas_call x1, Pallas kernels, radiance_call(): pl.pallas_call(radiance_kernel, out_shape=jax.ShapeDtypeStruct((4 * OWNER...  34.7 us
    pallas_call x1, Pallas kernels, exchange_call(): pl.pallas_call(exchange_kernel, out_shape=jax.ShapeDtypeStruct(blocks.sha...  20.7 us
    pallas_call x1, Pallas kernels, film_call(): pl.pallas_call(film_kernel, out_shape=jax.ShapeDtypeStruct((3, 8, 256), F...  5.67 us
    ppermute x1, starting transfers between devices, per_device(): yhi = lax.ppermute(yface(0), 'by', down)  4.54 us
    ppermute x1, starting transfers between devices, per_device(): lax.ppermute(masked(photon_data[:, CX - 1], block_counts[CX - 1]), 'bx', up)  3.08 us
    slice x2, local copies, waits for them, and re-layouts, masked(): return jnp.concatenate([x[None], face[1:]], axis=0)  2.92 us
  transfers between devices with their start and end apart: 4, of which 0 were waited for; matrix products, arithmetic and copies ran while one was open for 13% of the time, Pallas kernels for 0%

profile of v1, /device:TPU:1, one launch (start us, length us, event | category | flops | bytes accessed | tf_op | source)
XLA Modules:
  0.0 84.7 jit_solution(1327751051768377186)
XLA Ops:
  0.0 1.0 %slice_reduce_fusion.1 = (s32[32]{0:T(128)S(1)}, s32[32]{0:T(128)S(1)}) fusion(s32[64,32]{0,1:T(8,128)} %param.8), kind=kLoop, calls=%fused_computation.42 | loop fusion | bytes 512 | tf_op jit(solution)/shard_map/slice | solution.py:280
  1.0 0.9 %slice_bitcast_fusion.1 = (f32[5,32,128]{2,1,0:T(8,128)S(1)}, f32[5,32,128]{2,1,0:T(8,128)S(1)}) fusion(f32[6,64,32,128]{3,2,1,0:T(8,128)} %ph.1), kind=kLoop, calls=%fused_computation.18 | loop fusion | bytes 327680 | tf_op jit(solution)/shard_map/slice | solution.py:277
  1.9 0.8 bitcast_select_fusion.1
  2.8 3.1 %collective-permute-start = (f32[6,32,128]{2,1,0:T(8,128)S(1)}, f32[6,32,128]{2,1,0:T(8,128)S(1)}, u32[]{:S(2)}, u32[]{:S(2)}) collective-permute-start(f32[6,32,128]{2,1,0:T(8,128)S(1)} %pad_maximum_fusion.4), channel_id=1, source_target_pairs={{0,8},{8,16},{16,24},{24,32},{32,40},{40,48},{48,56},{56,64},{64,7... | collective-permute-start | bytes 294920 | tf_op jit(solution)/shard_map/ppermute | solution.py:280
  5.8 0.1 collective-permute-start.1
  5.9 1.1 %fusion.13 = (f32[1,64,1,128]{3,2,1,0:T(1,128)S(1)}, f32[1,64,1,128]{3,2,1,0:T(1,128)S(1)}) fusion(f32[6,64,32,128]{3,2,1,0:T(8,128)} %ph.1), kind=kLoop, calls=%fused_computation.49 | loop fusion | bytes 131072 | tf_op jit(solution)/shard_map/slice | solution.py:276
  7.0 0.7 slice_bitcast_fusion.3
  7.7 2.0 %fusion.14 = (f32[5,64,1,128]{3,2,1,0:T(1,128)S(1)}, f32[5,64,1,128]{3,2,1,0:T(1,128)S(1)}) fusion(f32[6,64,32,128]{3,2,1,0:T(8,128)} %ph.1), kind=kLoop, calls=%fused_computation.50 | loop fusion | bytes 655360 | tf_op jit(solution)/shard_map/slice | solution.py:277
  9.7 0.1 fusion.7
  9.8 0.1 fusion.8
  9.9 1.2 %fusion.11 = (s32[4096]{0:T(1024)S(1)}, s32[4,4096]{1,0:T(4,128)S(1)}, s32[4096]{0:T(1024)S(1)}, s32[4,4096]{1,0:T(4,128)S(1)}) fusion(s32[]{:T(128)S(6)} %mul.24, s32[4,4096]{1,0:T(4,128)} %param.10, s32[]{:T(128)S(6)} %mul.27), kind=kLoop, calls=%fused_computation.47 | loop fusion | flops 761856 | bytes 229384 | tf_op jit(solution)/shard_map/reduce_min | solution.py:292
  11.0 1.0 %fusion.10 = (f32[1,4096]{1,0:T(1,128)S(1)}, f32[1,4096]{1,0:T(1,128)S(1)}, f32[1,4096]{1,0:T(1,128)S(1)}) fusion(s32[4,4096]{1,0:T(4,128)S(1)} %get-tuple-element.8, f32[3,4096]{1,0:T(4,128)} %param.9, s32[4,4096]{1,0:T(4,128)S(1)} %get-tuple-element.27), kind=kLoop, calls=%fused_computation.37 | loop fusion | flops 16384 | bytes 131072 | tf_op jit(solution)/shard_map/add | solution.py:294
  12.1 0.6 maximum_multiply_fusion.off
  12.7 0.0 collective-permute-done
  12.7 0.0 collective-permute-done.1
  12.8 1.4 %collective-permute-start.2 = (f32[6,66,128]{2,1,0:T(8,128)S(1)}, f32[6,66,128]{2,1,0:T(8,128)S(1)}, u32[]{:S(2)}, u32[]{:S(2)}) collective-permute-start(f32[6,66,128]{2,1,0:T(8,128)S(1)} %pad_maximum_fusion.1), channel_id=1, source_target_pairs={{0,1},{1,2},{2,3},{3,4},{4,5},{5,6},{6,7},{7,0},{8,9},{9,10},{10,1... | collective-permute-start | bytes 608264 | tf_op jit(solution)/shard_map/ppermute | solution.py:288
  14.1 4.5 %collective-permute-start.3 = (f32[6,66,128]{2,1,0:T(8,128)S(1)}, f32[6,66,128]{2,1,0:T(8,128)S(1)}, u32[]{:S(2)}, u32[]{:S(2)}) collective-permute-start(f32[6,66,128]{2,1,0:T(8,128)S(1)} %pad_maximum_fusion.2), channel_id=1, source_target_pairs={{1,0},{2,1},{3,2},{4,3},{5,4},{6,5},{7,6},{0,7},{9,8},{10,9},{11,1... | collective-permute-start | bytes 608264 | tf_op jit(solution)/shard_map/ppermute | solution.py:289
  18.7 0.6 multiply_add_fusion.idx
  19.3 0.7 convert_element_type.13
  20.0 1.5 %copy.37 = f32[1,3,32,128]{3,2,1,0:T(8,128)} copy(f32[1,3,32,128]{3,1,2,0:T(4,128)} %bitcast.54) | data formatting | bytes 98304
  21.5 0.7 copy.28.cnt
  22.2 0.7 pad_maximum_fusion.3.xf
  22.9 0.0 collective-permute-done.2
  22.9 0.0 collective-permute-done.3
  22.9 0.8 pad_maximum_fusion.yf
  23.7 34.7 %radiance.1 = f32[512,128]{1,0:T(8,128)} custom-call(s32[4096]{0:T(1024)} %multiply_add_fusion.idx, f32[12288]{0:T(1024)} %maximum_multiply_fusion.off, f32[6,64,32,128]{3,2,1,0:T(8,128)} %ph.1, f32[64,32]{1,0:T(8,128)} %copy.28.cnt, f32[2,6,32,128]{3,2,1,0:T(8,128)} %pad_maximum_fusion.3.xf, f32[2,6,66,128]{3,2,1,0:T(8,128)} %pad_maximum_fusion.yf, ...), custom_call_target="tpu_custom_call" | custom-call | tf_op jit(solution)/shard_map/radiance/pallas_call | solution.py:163
  58.4 20.7 %exchange.1 = f32[128,4,128]{2,1,0:T(4,128)} custom-call(f32[128,4,128]{2,1,0:T(4,128)} %bitcast.43), custom_call_target="tpu_custom_call" | custom-call | tf_op jit(solution)/shard_map/exchange/pallas_call | solution.py:254
  79.0 5.7 %film.1 = f32[3,8,256]{2,1,0:T(8,128)} custom-call(f32[512,128]{1,0:T(8,128)} %bitcast.44), custom_call_target="tpu_custom_call" | custom-call | tf_op jit(solution)/shard_map/film/pallas_call | solution.py:207
  (6 shorter events, 0.1 us)
Async XLA Ops:
  2.8 9.9 %collective-permute-start = (f32[6,32,128]{2,1,0:T(8,128)S(1)}, f32[6,32,128]{2,1,0:T(8,128)S(1)}, u32[]{:S(2)}, u32[]{:S(2)}) collective-permute-start(f32[6,32,128]{2,1,0:T(8,128)S(1)} %pad_maximum_fusion.4), channel_id=1, source_target_pairs={{0,8},{8,16},{16,24},{24,32},{32,40},{40,48},{48,56},{56,64},{64,7... | collective-permute-start | bytes 294920 | tf_op jit(solution)/shard_map/ppermute | solution.py:280
  5.8 6.9 %collective-permute-start.1 = (f32[6,32,128]{2,1,0:T(8,128)S(1)}, f32[6,32,128]{2,1,0:T(8,128)S(1)}, u32[]{:S(2)}, u32[]{:S(2)}) collective-permute-start(f32[6,32,128]{2,1,0:T(8,128)S(1)} %pad_maximum_fusion.5), channel_id=1, source_target_pairs={{8,0},{16,8},{24,16},{32,24},{40,32},{48,40},{56,48},{64,56},{72,6... | collective-permute-start | bytes 294920 | tf_op jit(solution)/shard_map/ppermute | solution.py:281
  12.8 10.1 %collective-permute-start.2 = (f32[6,66,128]{2,1,0:T(8,128)S(1)}, f32[6,66,128]{2,1,0:T(8,128)S(1)}, u32[]{:S(2)}, u32[]{:S(2)}) collective-permute-start(f32[6,66,128]{2,1,0:T(8,128)S(1)} %pad_maximum_fusion.1), channel_id=1, source_target_pairs={{0,1},{1,2},{2,3},{3,4},{4,5},{5,6},{6,7},{7,0},{8,9},{9,10},{10,1... | collective-permute-start | bytes 608264 | tf_op jit(solution)/shard_map/ppermute | solution.py:288
  14.1 8.7 %collective-permute-start.3 = (f32[6,66,128]{2,1,0:T(8,128)S(1)}, f32[6,66,128]{2,1,0:T(8,128)S(1)}, u32[]{:S(2)}, u32[]{:S(2)}) collective-permute-start(f32[6,66,128]{2,1,0:T(8,128)S(1)} %pad_maximum_fusion.2), channel_id=1, source_target_pairs={{1,0},{2,1},{3,2},{4,3},{5,4},{6,5},{7,6},{0,7},{9,8},{10,9},{11,1... | collective-permute-start | bytes 608264 | tf_op jit(solution)/shard_map/ppermute | solution.py:289

commit v2 on v0

v2 whole, which is shorter than its diff:
```python
import jax
import jax.numpy as jnp
from jax import lax
from jax.experimental import pallas as pl
from jax.experimental.pallas import tpu as pltpu
from jax.sharding import PartitionSpec as P

MESH = pl.DeviceIdType.MESH
F32, BF16, I32 = jnp.float32, jnp.bfloat16, jnp.int32
NX, NY = 16, 8
N = NX * NY
CX, CY, SLOTS, G = 64, 32, 128, 4096
NXC, NYC = 1024, 256
PITCH = 2 * (CY + 2)
PAD = 8
NR = 4456
RANKS = 96
FAR = 1.0e9
GROUPS = G // 128
FACES = ((1, 0), (-1, 0), (0, 1), (0, -1), (1, 1), (1, -1), (-1, 1), (-1, -1))


def iota(shape, dim):
    return lax.broadcasted_iota(I32, shape, dim)


def hot(mask):
    return mask.astype(F32).astype(BF16)


def split(x):
    high = x.astype(BF16).astype(F32)
    return high, x - high


def across(a, b):
    return lax.dot_general(a, b, (((1,), (1,)), ((), ())), preferred_element_type=F32)


def peer_of(flat):
    return (flat >> 3, flat & 7)


def greet_all(me):
    barrier = pltpu.get_barrier_semaphore()

    def greet(k, unused):
        pl.semaphore_signal(barrier, inc=1, device_id=peer_of((me + k) & (N - 1)), device_id_type=MESH)
        return unused

    lax.fori_loop(1, N, greet, 0)
    return barrier


def prepare(blocks, goff, ix, iy, rowv):
    cells = blocks[...]
    lx = ((cells >> 8) - ix * CX + 1) & (NXC - 1)
    ly = ((cells & (NYC - 1)) - iy * CY + 1) & (NYC - 1)
    x = jnp.minimum(jnp.min(lx, axis=0, keepdims=True), CX)
    y = jnp.minimum(jnp.min(ly, axis=0, keepdims=True), CY)
    rowv[0][...] = PAD + PITCH * x + 2 * y
    rowv[1][...] = 2.0 * (lx[0:1].astype(F32) + goff[0:1, :])
    rowv[2][...] = 2.0 * (ly[0:1].astype(F32) + goff[1:2, :])
    rowv[3][...] = 2.0 * goff[2:3, :]


def spread_counts(cnt, cb):
    eye = iota((CY, CY), 0) == iota((CY, CY), 1)
    counts = cnt[...].astype(F32)
    spread = jnp.where(eye[None], counts[:, None, :], 0.0).reshape(CX * CY, CY)
    cb[...] = jnp.dot(spread.astype(BF16), jnp.ones((CY, SLOTS), BF16), preferred_element_type=F32)


def change(c, v, x, y):
    if c == 0:
        return 2.0 * (v + x)
    if c == 1:
        return 2.0 * (v + y)
    return 2.0 * v if c == 2 else v


def build_faces(ph, cb, fx, fy, fc):
    slot = iota((8, SLOTS), 1).astype(F32)
    sub = iota((8, SLOTS), 0).astype(F32)

    def cell(c, row, rows, stride, x, y):
        at = pl.ds(row, rows, stride=stride) if rows > 1 else pl.ds(row, 1)
        v = change(c, ph[c, at, :], x, y)
        return jnp.where(slot[:rows] < cb[at, :], v, FAR) if c == 0 else v

    for side, (x, to) in enumerate(((CX - 1, 0.0), (0, CX + 1.0))):
        for c in range(6):
            for n in range(CY // 8):
                fx[side, c, 8 * n : 8 * n + 8, :] = cell(c, x * CY + 8 * n, 8, 1, to, sub + (1.0 + 8 * n))
    for side, (y, to) in enumerate(((CY - 1, 0.0), (0, CY + 1.0))):
        for c in range(6):
            for n in range(CX // 8):
                fy[side, c, 8 * n : 8 * n + 8, :] = cell(c, 8 * n * CY + y, 8, CY, sub + (1.0 + 8 * n), to)
    for k, (dx, dy) in enumerate(FACES[4:]):
        x, tx = (CX - 1, 0.0) if dx > 0 else (0, CX + 1.0)
        y, ty = (CY - 1, 0.0) if dy > 0 else (0, CY + 1.0)
        for c in range(6):
            fc[k, c : c + 1, :] = cell(c, x * CY + y, 1, 1, tx, ty)


def build_own(ph, cb, table):
    slot = iota((8, SLOTS), 1).astype(F32)
    sub = iota((8, SLOTS), 0).astype(F32)

    def one_x(x, unused):
        xs = (x + 1).astype(F32)
        for n in range(CY // 8):
            at = pl.ds(pl.multiple_of(x * CY + 8 * n, 8), 8)
            live = slot < cb[at, :]
            for c in range(6):
                v = change(c, ph[c, at, :], xs, sub + (1.0 + 8 * n))
                if c == 0:
                    v = jnp.where(live, v, FAR)
                base = c * NR + PAD + (x + 1) * PITCH + 2 * (1 + 8 * n)
                table[pl.ds(base, 8, stride=2), :] = v
                table[pl.ds(base - PITCH + 1, 8, stride=2), :] = v
        return unused

    lax.fori_loop(0, CX, one_x, 0)


def build_halo(rx, ry, rc, table):
    for c in range(6):
        for side, base in enumerate((c * NR + PAD, c * NR + PAD + CX * PITCH + 1)):
            for n in range(CY // 8):
                table[pl.ds(base + 2 + 16 * n, 8, stride=2), :] = rx[side, c, 8 * n : 8 * n + 8, :]
        for side, y in enumerate((0, CY + 1)):
            for n in range(CX // 8):
                v = ry[side, c, 8 * n : 8 * n + 8, :]
                base = c * NR + PAD + (8 * n + 1) * PITCH + 2 * y
                table[pl.ds(base, 8, stride=PITCH), :] = v
                table[pl.ds(base - PITCH + 1, 8, stride=PITCH), :] = v
        for k, (dx, dy) in enumerate(FACES[4:]):
            y = 0 if dy > 0 else CY + 1
            base = c * NR + PAD + (0 if dx > 0 else CX * PITCH + 1) + 2 * y
            table[pl.ds(base, 1), :] = rc[k, c : c + 1, :]


def rank_points(pix, ts, em, rt, lhs, carry):
    t = ts[...]
    lookup = jnp.concatenate([t >> 3, t & 7], axis=0).astype(F32).astype(BF16)
    rows, cols = iota((128, 128), 0), iota((128, 128), 1)
    before = jnp.concatenate([hot(rows < cols), jnp.ones((128, 128), BF16)], axis=1)
    eight = iota((8, 128), 0)
    carry[...] = jnp.zeros((128, 128), F32)

    def tiles(i, unused):
        for u in range(4):
            j = 4 * i + u
            at = pl.ds(pl.multiple_of(j * 128, 128), 128)
            pixel = pix[pl.ds(j, 1), :]
            image = pixel >> 8
            found = jnp.dot(lookup, hot(rows == (image & 127)), preferred_element_type=F32)
            pick = eight == (image >> 7)
            owner = jnp.sum(jnp.where(pick, found[:8], 0.0), axis=0, keepdims=True)
            inner = jnp.sum(jnp.where(pick, found[8:], 0.0), axis=0, keepdims=True)
            mine = rows == owner.astype(I32)
            chosen = hot(mine)
            em[:, at] = chosen
            counts = jnp.dot(chosen, before, preferred_element_type=F32)
            rank = jnp.sum(jnp.where(mine, counts[:, :128] + carry[...], 0.0), axis=0, keepdims=True)
            carry[...] += counts[:, 128:]
            place = hot(rows == rank.astype(I32))[:RANKS]
            rt[:, at] = place
            local = inner * 256.0 + (pixel & 255).astype(F32)
            high = jnp.floor(local * (1.0 / 128.0))
            lhs[0:RANKS, at] = place * high.astype(BF16)
            lhs[RANKS : 2 * RANKS, at] = place * (local - 128.0 * high).astype(BF16)
        return unused

    lax.fori_loop(0, GROUPS // 4, tiles, 0)


def by_owner(part):
    whole = jnp.concatenate([part, jnp.zeros((128 - RANKS, 128), F32)], axis=0)
    return whole.T


def pack_pixels(em, lhs, psend):
    part = across(lhs[0 : 2 * RANKS, :], em[...])
    psend.reshape(N, 128)[...] = by_owner(128.0 * part[:RANKS] + part[RANKS:])


def weigh_tile(j, idx, off, table, prod, sums):
    half = iota((8, SLOTS), 0) < 4
    for u in range(16):
        g0 = j * 128 + 8 * u
        for pair in range(4):
            p, q = g0 + 2 * pair, g0 + 2 * pair + 1
            rp, rq = idx[0, p], idx[0, q] - 4
            v = []
            for c in range(6):
                a = table[pl.ds(rp + c * NR, 8), :]
                b = table[pl.ds(rq + c * NR, 8), :]
                if c < 3:
                    a, b = a - off[c][0, p], b - off[c][0, q]
                v.append(jnp.where(half, a, b))
            w = jnp.maximum(1.0 - (v[0] * v[0] + v[1] * v[1] + v[2] * v[2]), 0.0)
            for c in range(3):
                prod[c, u, 8 * pair : 8 * pair + 8, :] = w * v[3 + c]
        for c in range(3):
            s = [prod[c, u, pl.ds(k, 8, stride=4), :] for k in range(4)]
            sums[c, 8 * u : 8 * u + 8, :] = (s[0] + s[1]) + (s[2] + s[3])


def place_tile(j, alb, sums, rt, lhs):
    at = pl.ds(pl.multiple_of(j * 128, 128), 128)
    ones = jnp.ones((8, 256), BF16)
    place = rt[:, at]
    for c in range(3):
        whole = sums[c]
        high = whole.astype(BF16)
        low = (whole - high.astype(F32)).astype(BF16)
        total = across(ones, jnp.concatenate([high, low], axis=1))
        for k, row in enumerate(split(total[0:1] * alb[c : c + 1, at])):
            first = RANKS * (2 * c + k)
            lhs[first : first + RANKS, at] = place * row.astype(BF16)


def radiance(idx, off, table, prod, sums, alb, rt, lhs):
    def tile(j, unused):
        place_tile(jnp.maximum(j - 1, 0), alb, sums, rt, lhs)
        weigh_tile(j, idx, off, table, prod, sums)
        return unused

    sums[...] = jnp.zeros((3, 128, SLOTS), F32)
    lax.fori_loop(0, GROUPS, tile, 0)
    place_tile(GROUPS - 1, alb, sums, rt, lhs)


def pack(em, lhs, send):
    part = across(lhs[...], em[...])
    flat = send.reshape(4 * N, 128)
    for c in range(3):
        a = part[2 * c * RANKS : (2 * c + 1) * RANKS]
        b = part[(2 * c + 1) * RANKS : (2 * c + 2) * RANKS]
        flat[pl.ds(c, 128, stride=4), :] = by_owner(a + b)


def spot_pixels(pgot, spot, rt):
    rows = iota((128, 128), 0)
    sixteen = iota((16, 128), 0)

    def sources(i, unused):
        for u in range(4):
            s = 4 * i + u
            at = pl.ds(pl.multiple_of(s * 128, 128), 128)
            pixel = pgot[s].astype(I32)
            rt[:, at] = hot(rows == (pixel & 127))
            spot[:, at] = hot(sixteen == ((pixel >> 7) & 1) * 8 + (pixel >> 8))
        return unused

    lax.fori_loop(0, N // 4, sources, 0)


def film_of(got, film, spot, lhs, rt):
    def sources(i, unused):
        for u in range(4):
            s = 4 * i + u
            at = pl.ds(pl.multiple_of(s * 128, 128), 128)
            entry = got[s]
            where = spot[:, at]
            for c in range(3):
                for k, part in enumerate(split(entry[c : c + 1, :])):
                    first = 16 * (2 * c + k)
                    lhs[first : first + 16, at] = where * part.astype(BF16)
        return unused

    lax.fori_loop(0, N // 4, sources, 0)
    total = across(lhs[...], rt[...])
    for c in range(3):
        both = total[32 * c : 32 * c + 16] + total[32 * c + 16 : 32 * c + 32]
        film[c, :, 0:128] = both[:8]
        film[c, :, 128:256] = both[8:]


def ship_all(me, send, got, own_sem, send_sem, recv_sem):
    own = pltpu.make_async_copy(send.at[pl.ds(me, 1)], got.at[pl.ds(me, 1)], own_sem)
    own.start()

    def ship(k, unused):
        peer = (me + k) & (N - 1)
        pltpu.make_async_remote_copy(
            src_ref=send.at[pl.ds(peer, 1)],
            dst_ref=got.at[pl.ds(me, 1)],
            send_sem=send_sem,
            recv_sem=recv_sem,
            device_id=peer_of(peer),
            device_id_type=MESH,
        ).start()
        return unused

    lax.fori_loop(1, N, ship, 0)
    return own


def wait_all(own, send, got, send_sem, recv_sem):
    own.wait()
    for sem in (recv_sem, send_sem):
        pltpu.make_async_copy(send.at[pl.ds(0, N - 1)], got.at[pl.ds(0, N - 1)], sem).wait()


def kernel(
    blocks, goff, photons, cnt, alb, pix, ts, film,
    ph, table, cb, idxv, oxv, oyv, ozv, idx, ox, oy, oz, prod, sums, em, rt, lhs, carry,
    fx, fy, fc, rx, ry, rc, psend, pgot, send, got, spot, flhs, frt,
    ph_sem, idx_sem, own_sem, face_send, face_recv, send_sem, recv_sem, pown_sem, psend_sem, precv_sem,
):
    ix, iy = lax.axis_index("bx"), lax.axis_index("by")
    me = ix * NY + iy
    load = pltpu.make_async_copy(photons, ph, ph_sem)
    load.start()
    barrier = greet_all(me)
    rowv, row = (idxv, oxv, oyv, ozv), (idx, ox, oy, oz)
    prepare(blocks, goff, ix, iy, rowv)
    rows = [pltpu.make_async_copy(v, r, idx_sem.at[k]) for k, (v, r) in enumerate(zip(rowv, row))]
    for copy in rows:
        copy.start()
    spread_counts(cnt, cb)
    load.wait()
    build_faces(ph, cb, fx, fy, fc)
    build_own(ph, cb, table)
    pl.semaphore_wait(barrier, N - 1)
    copies = []
    for k, (dx, dy) in enumerate(FACES):
        source, target = ((fx, rx), (fy, ry), (fc, rc))[min(k // 2, 2)]
        k2 = k % 2 if k < 4 else k - 4
        copy = pltpu.make_async_remote_copy(
            src_ref=source.at[k2],
            dst_ref=target.at[k2],
            send_sem=face_send.at[k],
            recv_sem=face_recv.at[k],
            device_id=((ix + dx) & (NX - 1), (iy + dy) & (NY - 1)),
            device_id_type=MESH,
        )
        copies.append(copy)
    for k in (2, 3, 0, 1, 4, 5, 6, 7):
        copies[k].start()
    rank_points(pix, ts, em, rt, lhs, carry)
    pack_pixels(em, lhs, psend)
    pown = ship_all(me, psend, pgot, pown_sem, psend_sem, precv_sem)
    for copy in rows:
        copy.wait()
    for copy in copies:
        copy.wait()
    build_halo(rx, ry, rc, table)
    radiance(idx, (ox, oy, oz), table, prod, sums, alb, rt, lhs)
    pack(em, lhs, send)
    own = ship_all(me, send, got, own_sem, send_sem, recv_sem)
    wait_all(pown, psend, pgot, psend_sem, precv_sem)
    spot_pixels(pgot, spot, frt)
    wait_all(own, send, got, send_sem, recv_sem)
    film_of(got, film, spot, flhs, frt)


def per_device(photon_data, block_counts, gather_offsets, gather_blocks, albedo, gather_pixels, tile_slot):
    vmem = pl.BlockSpec(memory_space=pltpu.VMEM)
    dma = pltpu.SemaphoreType.DMA
    return pl.pallas_call(
        kernel,
        out_shape=jax.ShapeDtypeStruct((3, 8, 256), F32),
        in_specs=[vmem, vmem, pl.BlockSpec(memory_space=pl.ANY), vmem, vmem, vmem, vmem],
        out_specs=vmem,
        scratch_shapes=[
            pltpu.VMEM((6, CX * CY, SLOTS), F32),
            pltpu.VMEM((6 * NR, SLOTS), F32),
            pltpu.VMEM((CX * CY, SLOTS), F32),
            pltpu.VMEM((1, G), I32),
            pltpu.VMEM((1, G), F32),
            pltpu.VMEM((1, G), F32),
            pltpu.VMEM((1, G), F32),
            pltpu.SMEM((1, G), I32),
            pltpu.SMEM((1, G), F32),
            pltpu.SMEM((1, G), F32),
            pltpu.SMEM((1, G), F32),
            pltpu.VMEM((3, 16, 32, SLOTS), F32),
            pltpu.VMEM((3, 128, SLOTS), F32),
            pltpu.VMEM((128, G), BF16),
            pltpu.VMEM((RANKS, G), BF16),
            pltpu.VMEM((6 * RANKS, G), BF16),
            pltpu.VMEM((128, 128), F32),
            pltpu.VMEM((2, 6, CY, SLOTS), F32),
            pltpu.VMEM((2, 6, CX, SLOTS), F32),
            pltpu.VMEM((4, 8, SLOTS), F32),
            pltpu.VMEM((2, 6, CY, SLOTS), F32),
            pltpu.VMEM((2, 6, CX, SLOTS), F32),
            pltpu.VMEM((4, 8, SLOTS), F32),
            pltpu.VMEM((N, 1, 128), F32),
            pltpu.VMEM((N, 1, 128), F32),
            pltpu.VMEM((N, 4, 128), F32),
            pltpu.VMEM((N, 4, 128), F32),
            pltpu.VMEM((16, N * 128), BF16),
            pltpu.VMEM((96, N * 128), BF16),
            pltpu.VMEM((128, N * 128), BF16),
            dma, dma((4,)), dma, dma((8,)), dma((8,)), dma, dma, dma, dma, dma,
        ],
        compiler_params=pltpu.CompilerParams(
            vmem_limit_bytes=67043328, collective_id=1, has_side_effects=True
        ),
        name="photon_film",
    )(
        gather_blocks,
        gather_offsets,
        photon_data.reshape(6, CX * CY, SLOTS),
        block_counts,
        albedo,
        gather_pixels.reshape(GROUPS, 128),
        tile_slot.reshape(8, 128),
    )


def solution(mesh):
    in_specs = (
        P(None, "bx", "by", None),
        P("bx", "by"),
        P(None, ("bx", "by")),
        P(None, ("bx", "by")),
        P(None, ("bx", "by")),
        P(("bx", "by")),
        P(),
    )
    out_specs = P(None, ("bx", "by"), None)
    return jax.shard_map(per_device, mesh=mesh, in_specs=in_specs, out_specs=out_specs, check_vma=False)
```

time: 1030 us -> 52.6 us (0.05); the launches traced: 1020 us -> 52.3 us
  local copies, waits for them, and re-layouts: 373 us -> 2.75 us
  waiting for transfers between devices: 288 us -> 0 us
  other arithmetic: 279 us -> 0 us
  Pallas kernels: 0 us -> 49.5 us
  blocking collectives: 37.5 us -> 0 us
  between operations: 27.4 us -> 0.01 us
    unnamed x16 -> x0, waiting for transfers between devices: 285 us -> none
    gather x8 -> x0, local copies, waits for them, and re-layouts: 156 us -> none  [one_group(): jnp.take(table, idb.reshape(-1), axis=1).reshape(6, group, listed, slots)]
    scatter-add x3 -> x0, other arithmetic: 103 us -> none  [per_device(): jnp.zeros((3, tiles * TILE_PIX), jnp.float32).at[:, target].add(radiance)]
    select_n x18 -> x0, other arithmetic: 90.4 us -> none  [the longest x16 89.7 us: one_group(): jnp.take(table, idb.reshape(-1), axis=1).reshape(6, group, listed, slots)]
    another operation x1 -> x0, local copies, waits for them, and re-layouts: 69.1 us -> none  [cut_along(): return jnp.moveaxis(x.reshape(*before, peers, -1, *after), dim, 0)]
    reduce_sum x17 -> x0, other arithmetic: 55.3 us -> none  [the longest x16 51.5 us: kernel_sum(): sums = jnp.sum(weight[None] * blocks[3:6], axis=(2, 3))]
    pallas_call x0 -> x1, Pallas kernels: none -> 49.5 us  [per_device(): pl.pallas_call(kernel, out_shape=jax.ShapeDtypeStruct((3, 8, 256), F32),...]
    unnamed x4 -> x0, blocking collectives: 37.5 us -> none
  transfers between devices with their start and end apart: 12 -> 0, of which waited for: 9 -> 0; matrix products, arithmetic and copies ran while one was open for 3% -> 0% of each run, Pallas kernels for 0% -> 0%
where the time goes in v2:
time: 52.6 us; the launch traced here: 52.3 us
  Pallas kernels  49.5 us (94%)
  local copies, waits for them, and re-layouts  2.75 us (5%)
    pallas_call x1, Pallas kernels, per_device(): pl.pallas_call(kernel, out_shape=jax.ShapeDtypeStruct((3, 8, 256), F32),...  49.5 us
    unnamed x2, local copies, waits for them, and re-layouts  2.75 us

profile of v2, /device:TPU:1, one launch (start us, length us, event | category | flops | bytes accessed | tf_op | source)
XLA Modules:
  0.0 52.3 jit_solution(402131511368482553)
XLA Ops:
  0.0 1.4 %copy.8.cnt = s32[64,32]{1,0:T(8,128)} copy(s32[64,32]{0,1:T(8,128)} %param.8) | data formatting | bytes 16384 | tf_op args[1]
  1.4 49.5 %photon_film.1 = f32[3,8,256]{2,1,0:T(8,128)} custom-call(s32[4,4096]{1,0:T(4,128)} %blocks.1, f32[3,4096]{1,0:T(4,128)} %goff.1, f32[6,2048,128]{2,1,0:T(8,128)} %bitcast.3, s32[64,32]{1,0:T(8,128)} %copy.8.cnt, f32[3,4096]{1,0:T(4,128)} %alb.1, s32[32,128]{1,0:T(8,128)} %bitcast.4, s32[8,128]{1,0:T(8,128)} %bitcast.5), custom_call_target="tpu_custom_call" | custom-call | tf_op jit(solution)/shard_map/photon_film/pallas_call | solution.py:364
  50.9 1.3 %copy.10 = f32[3,8,256]{2,1,0:T(8,128)} copy(f32[3,8,256]{2,1,0:T(8,128)} %photon_film.1) | data formatting | bytes 49152

commit v3 on v2

--- a/solution.py
+++ b/solution.py
@@ -15,6 +15,7 @@
 PAD = 8
 NR = 4456
 RANKS = 96
+BLOCK = 32
 FAR = 1.0e9
 GROUPS = G // 128
 FACES = ((1, 0), (-1, 0), (0, 1), (0, -1), (1, 1), (1, -1), (-1, 1), (-1, -1))
@@ -65,10 +66,9 @@
 
 
 def spread_counts(cnt, cb):
-    eye = iota((CY, CY), 0) == iota((CY, CY), 1)
     counts = cnt[...].astype(F32)
-    spread = jnp.where(eye[None], counts[:, None, :], 0.0).reshape(CX * CY, CY)
-    cb[...] = jnp.dot(spread.astype(BF16), jnp.ones((CY, SLOTS), BF16), preferred_element_type=F32)
+    for x in range(CX):
+        cb[x * CY : x * CY + CY, :] = jnp.broadcast_to(counts[:, x : x + 1], (CY, SLOTS))
 
 
 def change(c, v, x, y):
@@ -258,7 +258,7 @@
     lax.fori_loop(0, N // 4, sources, 0)
 
 
-def film_of(got, film, spot, lhs, rt):
+def film_part(b, got, spot, lhs, rt, total):
     def sources(i, unused):
         for u in range(4):
             s = 4 * i + u
@@ -271,10 +271,14 @@
                     lhs[first : first + 16, at] = where * part.astype(BF16)
         return unused
 
-    lax.fori_loop(0, N // 4, sources, 0)
-    total = across(lhs[...], rt[...])
+    lax.fori_loop(b * (BLOCK // 4), (b + 1) * (BLOCK // 4), sources, 0)
+    at = pl.ds(pl.multiple_of(b * (BLOCK * 128), 128), BLOCK * 128)
+    total[...] += across(lhs[:, at], rt[:, at])
+
+
+def film_of(film, total):
     for c in range(3):
-        both = total[32 * c : 32 * c + 16] + total[32 * c + 16 : 32 * c + 32]
+        both = total[32 * c : 32 * c + 16, :] + total[32 * c + 16 : 32 * c + 32, :]
         film[c, :, 0:128] = both[:8]
         film[c, :, 128:256] = both[8:]
 
@@ -295,7 +299,8 @@
         ).start()
         return unused
 
-    lax.fori_loop(1, N, ship, 0)
+    for first in (64, 32, 96, 0):
+        lax.fori_loop(max(first, 1), first + 32, ship, 0)
     return own
 
 
@@ -308,23 +313,17 @@
 def kernel(
     blocks, goff, photons, cnt, alb, pix, ts, film,
     ph, table, cb, idxv, oxv, oyv, ozv, idx, ox, oy, oz, prod, sums, em, rt, lhs, carry,
-    fx, fy, fc, rx, ry, rc, psend, pgot, send, got, spot, flhs, frt,
-    ph_sem, idx_sem, own_sem, face_send, face_recv, send_sem, recv_sem, pown_sem, psend_sem, precv_sem,
+    fx, fy, fc, rx, ry, rc, psend, pgot, send, got, spot, flhs, frt, total,
+    ph_sem, idx_sem, face_send, face_recv, send_sem, recv_sem, pown_sem, psend_sem, precv_sem,
 ):
     ix, iy = lax.axis_index("bx"), lax.axis_index("by")
     me = ix * NY + iy
     load = pltpu.make_async_copy(photons, ph, ph_sem)
     load.start()
     barrier = greet_all(me)
-    rowv, row = (idxv, oxv, oyv, ozv), (idx, ox, oy, oz)
-    prepare(blocks, goff, ix, iy, rowv)
-    rows = [pltpu.make_async_copy(v, r, idx_sem.at[k]) for k, (v, r) in enumerate(zip(rowv, row))]
-    for copy in rows:
-        copy.start()
     spread_counts(cnt, cb)
     load.wait()
     build_faces(ph, cb, fx, fy, fc)
-    build_own(ph, cb, table)
     pl.semaphore_wait(barrier, N - 1)
     copies = []
     for k, (dx, dy) in enumerate(FACES):
@@ -341,9 +340,15 @@
         copies.append(copy)
     for k in (2, 3, 0, 1, 4, 5, 6, 7):
         copies[k].start()
+    rowv, row = (idxv, oxv, oyv, ozv), (idx, ox, oy, oz)
+    prepare(blocks, goff, ix, iy, rowv)
+    rows = [pltpu.make_async_copy(v, r, idx_sem.at[k]) for k, (v, r) in enumerate(zip(rowv, row))]
+    for copy in rows:
+        copy.start()
     rank_points(pix, ts, em, rt, lhs, carry)
     pack_pixels(em, lhs, psend)
     pown = ship_all(me, psend, pgot, pown_sem, psend_sem, precv_sem)
+    build_own(ph, cb, table)
     for copy in rows:
         copy.wait()
     for copy in copies:
@@ -351,11 +356,17 @@
     build_halo(rx, ry, rc, table)
     radiance(idx, (ox, oy, oz), table, prod, sums, alb, rt, lhs)
     pack(em, lhs, send)
-    own = ship_all(me, send, got, own_sem, send_sem, recv_sem)
+    quarter = me // BLOCK
+    own = ship_all(me, send, got, recv_sem.at[quarter], send_sem, recv_sem.at[quarter])
     wait_all(pown, psend, pgot, psend_sem, precv_sem)
     spot_pixels(pgot, spot, frt)
-    wait_all(own, send, got, send_sem, recv_sem)
-    film_of(got, film, spot, flhs, frt)
+    total[...] = jnp.zeros((96, 128), F32)
+    for step in (0, 1, 3, 2):
+        b = (quarter + step) & (N // BLOCK - 1)
+        pltpu.make_async_copy(send.at[pl.ds(0, BLOCK)], got.at[pl.ds(0, BLOCK)], recv_sem.at[b]).wait()
+        film_part(b, got, spot, flhs, frt, total)
+    film_of(film, total)
+    pltpu.make_async_copy(send.at[pl.ds(0, N - 1)], got.at[pl.ds(0, N - 1)], send_sem).wait()
 
 
 def per_device(photon_data, block_counts, gather_offsets, gather_blocks, albedo, gather_pixels, tile_slot):
@@ -397,7 +408,8 @@
             pltpu.VMEM((16, N * 128), BF16),
             pltpu.VMEM((96, N * 128), BF16),
             pltpu.VMEM((128, N * 128), BF16),
-            dma, dma((4,)), dma, dma((8,)), dma((8,)), dma, dma, dma, dma, dma,
+            pltpu.VMEM((96, 128), F32),
+            dma, dma((4,)), dma((8,)), dma((8,)), dma, dma((4,)), dma, dma, dma,
         ],
         compiler_params=pltpu.CompilerParams(
             vmem_limit_bytes=67043328, collective_id=1, has_side_effects=True
@@ -407,7 +419,7 @@
         gather_blocks,
         gather_offsets,
         photon_data.reshape(6, CX * CY, SLOTS),
-        block_counts,
+        block_counts.T,
         albedo,
         gather_pixels.reshape(GROUPS, 128),
         tile_slot.reshape(8, 128),

time: 52.6 us -> 49.6 us (0.943)
  Pallas kernels: 49.5 us -> 48 us
  local copies, waits for them, and re-layouts: 2.75 us -> 1.35 us
    pallas_call x1, Pallas kernels: 49.5 us -> 48 us  [per_device(): pl.pallas_call(kernel, out_shape=jax.ShapeDtypeStruct((3, 8, 256), F32),...]
    unnamed x2 -> x1, local copies, waits for them, and re-layouts: 2.75 us -> 1.35 us
where the time goes in v3:
time: 49.6 us; the launch traced here: 49.3 us
  Pallas kernels  48 us (97%)
  local copies, waits for them, and re-layouts  1.35 us (3%)
    pallas_call x1, Pallas kernels, per_device(): pl.pallas_call(kernel, out_shape=jax.ShapeDtypeStruct((3, 8, 256), F32),...  48 us
    unnamed x1, local copies, waits for them, and re-layouts  1.35 us

profile of v3, /device:TPU:1, one launch (start us, length us, event | category | flops | bytes accessed | tf_op | source)
XLA Modules:
  0.0 49.3 jit_solution(7246849419955587850)
XLA Ops:
  0.0 48.0 %photon_film.1 = f32[3,8,256]{2,1,0:T(8,128)} custom-call(s32[4,4096]{1,0:T(4,128)} %blocks.1, f32[3,4096]{1,0:T(4,128)} %goff.1, f32[6,2048,128]{2,1,0:T(8,128)} %bitcast.4, s32[32,64]{1,0:T(8,128)} %bitcast.5, f32[3,4096]{1,0:T(4,128)} %alb.1, s32[32,128]{1,0:T(8,128)} %bitcast.6, s32[8,128]{1,0:T(8,128)} %bitcast.7), custom_call_target="tpu_custom_call" | custom-call | tf_op jit(solution)/shard_map/photon_film/pallas_call | solution.py:375
  48.0 1.3 %copy.9 = f32[3,8,256]{2,1,0:T(8,128)} copy(f32[3,8,256]{2,1,0:T(8,128)} %photon_film.1) | data formatting | bytes 49152

commit v4 on v3

--- a/solution.py
+++ b/solution.py
@@ -79,28 +79,34 @@
     return 2.0 * v if c == 2 else v
 
 
-def build_faces(ph, cb, fx, fy, fc):
-    slot = iota((8, SLOTS), 1).astype(F32)
+def face_cell(ph, cb, c, row, rows, stride, x, y):
+    at = pl.ds(row, rows, stride=stride) if rows > 1 else pl.ds(row, 1)
+    v = change(c, ph[c, at, :], x, y)
+    slot = iota((rows, SLOTS), 1).astype(F32)
+    return jnp.where(slot < cb[at, :], v, FAR) if c == 0 else v
+
+
+def build_faces_y(ph, cb, fy, fc):
     sub = iota((8, SLOTS), 0).astype(F32)
-
-    def cell(c, row, rows, stride, x, y):
-        at = pl.ds(row, rows, stride=stride) if rows > 1 else pl.ds(row, 1)
-        v = change(c, ph[c, at, :], x, y)
-        return jnp.where(slot[:rows] < cb[at, :], v, FAR) if c == 0 else v
-
-    for side, (x, to) in enumerate(((CX - 1, 0.0), (0, CX + 1.0))):
-        for c in range(6):
-            for n in range(CY // 8):
-                fx[side, c, 8 * n : 8 * n + 8, :] = cell(c, x * CY + 8 * n, 8, 1, to, sub + (1.0 + 8 * n))
     for side, (y, to) in enumerate(((CY - 1, 0.0), (0, CY + 1.0))):
         for c in range(6):
             for n in range(CX // 8):
-                fy[side, c, 8 * n : 8 * n + 8, :] = cell(c, 8 * n * CY + y, 8, CY, sub + (1.0 + 8 * n), to)
+                v = face_cell(ph, cb, c, 8 * n * CY + y, 8, CY, sub + (1.0 + 8 * n), to)
+                fy[side, c, 8 * n : 8 * n + 8, :] = v
     for k, (dx, dy) in enumerate(FACES[4:]):
         x, tx = (CX - 1, 0.0) if dx > 0 else (0, CX + 1.0)
         y, ty = (CY - 1, 0.0) if dy > 0 else (0, CY + 1.0)
         for c in range(6):
-            fc[k, c : c + 1, :] = cell(c, x * CY + y, 1, 1, tx, ty)
+            fc[k, c : c + 1, :] = face_cell(ph, cb, c, x * CY + y, 1, 1, tx, ty)
+
+
+def build_faces_x(ph, cb, fx):
+    sub = iota((8, SLOTS), 0).astype(F32)
+    for side, (x, to) in enumerate(((CX - 1, 0.0), (0, CX + 1.0))):
+        for c in range(6):
+            for n in range(CY // 8):
+                v = face_cell(ph, cb, c, x * CY + 8 * n, 8, 1, to, sub + (1.0 + 8 * n))
+                fx[side, c, 8 * n : 8 * n + 8, :] = v
 
 
 def build_own(ph, cb, table):
@@ -223,23 +229,25 @@
 
 
 def radiance(idx, off, table, prod, sums, alb, rt, lhs):
-    def tile(j, unused):
-        place_tile(jnp.maximum(j - 1, 0), alb, sums, rt, lhs)
-        weigh_tile(j, idx, off, table, prod, sums)
-        return unused
-
-    sums[...] = jnp.zeros((3, 128, SLOTS), F32)
-    lax.fori_loop(0, GROUPS, tile, 0)
-    place_tile(GROUPS - 1, alb, sums, rt, lhs)
+    def tiles(i, unused):
+        place_tile(jnp.maximum(2 * i - 1, 0), alb, sums.at[1], rt, lhs)
+        weigh_tile(2 * i, idx, off, table, prod, sums.at[0])
+        place_tile(2 * i, alb, sums.at[0], rt, lhs)
+        weigh_tile(2 * i + 1, idx, off, table, prod, sums.at[1])
+        return unused
+
+    sums[...] = jnp.zeros((2, 3, 128, SLOTS), F32)
+    lax.fori_loop(0, GROUPS // 2, tiles, 0)
+    place_tile(GROUPS - 1, alb, sums.at[1], rt, lhs)
 
 
 def pack(em, lhs, send):
     part = across(lhs[...], em[...])
-    flat = send.reshape(4 * N, 128)
+    flat = send.reshape(3 * N, 128)
     for c in range(3):
         a = part[2 * c * RANKS : (2 * c + 1) * RANKS]
         b = part[(2 * c + 1) * RANKS : (2 * c + 2) * RANKS]
-        flat[pl.ds(c, 128, stride=4), :] = by_owner(a + b)
+        flat[pl.ds(c, 128, stride=3), :] = by_owner(a + b)
 
 
 def spot_pixels(pgot, spot, rt):
@@ -263,10 +271,9 @@
         for u in range(4):
             s = 4 * i + u
             at = pl.ds(pl.multiple_of(s * 128, 128), 128)
-            entry = got[s]
             where = spot[:, at]
             for c in range(3):
-                for k, part in enumerate(split(entry[c : c + 1, :])):
+                for k, part in enumerate(split(got[3 * s + c])):
                     first = 16 * (2 * c + k)
                     lhs[first : first + 16, at] = where * part.astype(BF16)
         return unused
@@ -283,15 +290,16 @@
         film[c, :, 128:256] = both[8:]
 
 
-def ship_all(me, send, got, own_sem, send_sem, recv_sem):
-    own = pltpu.make_async_copy(send.at[pl.ds(me, 1)], got.at[pl.ds(me, 1)], own_sem)
+def ship_all(me, rows, send, got, own_sem, send_sem, recv_sem):
+    here = pl.ds(me * rows, rows)
+    own = pltpu.make_async_copy(send.at[here], got.at[here], own_sem)
     own.start()
 
     def ship(k, unused):
         peer = (me + k) & (N - 1)
         pltpu.make_async_remote_copy(
-            src_ref=send.at[pl.ds(peer, 1)],
-            dst_ref=got.at[pl.ds(me, 1)],
+            src_ref=send.at[pl.ds(peer * rows, rows)],
+            dst_ref=got.at[here],
             send_sem=send_sem,
             recv_sem=recv_sem,
             device_id=peer_of(peer),
@@ -312,18 +320,23 @@
 
 def kernel(
     blocks, goff, photons, cnt, alb, pix, ts, film,
-    ph, table, cb, idxv, oxv, oyv, ozv, idx, ox, oy, oz, prod, sums, em, rt, lhs, carry,
+    ph4, table, cb, idxv, oxv, oyv, ozv, idx, ox, oy, oz, prod, sums, em, rt, lhs, carry,
     fx, fy, fc, rx, ry, rc, psend, pgot, send, got, spot, flhs, frt, total,
     ph_sem, idx_sem, face_send, face_recv, send_sem, recv_sem, pown_sem, psend_sem, precv_sem,
 ):
     ix, iy = lax.axis_index("bx"), lax.axis_index("by")
     me = ix * NY + iy
-    load = pltpu.make_async_copy(photons, ph, ph_sem)
-    load.start()
+    loads = []
+    for k, (first, last) in enumerate(((0, 8), (CY - 8, CY), (8, CY - 8))):
+        part = (slice(None), slice(None), pl.ds(first, last - first))
+        loads.append(pltpu.make_async_copy(photons.at[part], ph4.at[part], ph_sem.at[k]))
+        loads[k].start()
+    ph = ph4.reshape(6, CX * CY, SLOTS)
     barrier = greet_all(me)
     spread_counts(cnt, cb)
-    load.wait()
-    build_faces(ph, cb, fx, fy, fc)
+    loads[0].wait()
+    loads[1].wait()
+    build_faces_y(ph, cb, fy, fc)
     pl.semaphore_wait(barrier, N - 1)
     copies = []
     for k, (dx, dy) in enumerate(FACES):
@@ -338,7 +351,11 @@
             device_id_type=MESH,
         )
         copies.append(copy)
-    for k in (2, 3, 0, 1, 4, 5, 6, 7):
+    for k in (2, 3, 4, 5, 6, 7):
+        copies[k].start()
+    loads[2].wait()
+    build_faces_x(ph, cb, fx)
+    for k in (0, 1):
         copies[k].start()
     rowv, row = (idxv, oxv, oyv, ozv), (idx, ox, oy, oz)
     prepare(blocks, goff, ix, iy, rowv)
@@ -347,7 +364,7 @@
         copy.start()
     rank_points(pix, ts, em, rt, lhs, carry)
     pack_pixels(em, lhs, psend)
-    pown = ship_all(me, psend, pgot, pown_sem, psend_sem, precv_sem)
+    pown = ship_all(me, 1, psend, pgot, pown_sem, psend_sem, precv_sem)
     build_own(ph, cb, table)
     for copy in rows:
         copy.wait()
@@ -357,16 +374,18 @@
     radiance(idx, (ox, oy, oz), table, prod, sums, alb, rt, lhs)
     pack(em, lhs, send)
     quarter = me // BLOCK
-    own = ship_all(me, send, got, recv_sem.at[quarter], send_sem, recv_sem.at[quarter])
+    own = ship_all(me, 3, send, got, recv_sem.at[quarter], send_sem, recv_sem.at[quarter])
     wait_all(pown, psend, pgot, psend_sem, precv_sem)
     spot_pixels(pgot, spot, frt)
     total[...] = jnp.zeros((96, 128), F32)
     for step in (0, 1, 3, 2):
         b = (quarter + step) & (N // BLOCK - 1)
-        pltpu.make_async_copy(send.at[pl.ds(0, BLOCK)], got.at[pl.ds(0, BLOCK)], recv_sem.at[b]).wait()
+        quarter_rows = pl.ds(0, 3 * BLOCK)
+        pltpu.make_async_copy(send.at[quarter_rows], got.at[quarter_rows], recv_sem.at[b]).wait()
         film_part(b, got, spot, flhs, frt, total)
     film_of(film, total)
-    pltpu.make_async_copy(send.at[pl.ds(0, N - 1)], got.at[pl.ds(0, N - 1)], send_sem).wait()
+    sent = pl.ds(0, 3 * (N - 1))
+    pltpu.make_async_copy(send.at[sent], got.at[sent], send_sem).wait()
 
 
 def per_device(photon_data, block_counts, gather_offsets, gather_blocks, albedo, gather_pixels, tile_slot):
@@ -378,7 +397,7 @@
         in_specs=[vmem, vmem, pl.BlockSpec(memory_space=pl.ANY), vmem, vmem, vmem, vmem],
         out_specs=vmem,
         scratch_shapes=[
-            pltpu.VMEM((6, CX * CY, SLOTS), F32),
+            pltpu.VMEM((6, CX, CY, SLOTS), F32),
             pltpu.VMEM((6 * NR, SLOTS), F32),
             pltpu.VMEM((CX * CY, SLOTS), F32),
             pltpu.VMEM((1, G), I32),
@@ -390,7 +409,7 @@
             pltpu.SMEM((1, G), F32),
             pltpu.SMEM((1, G), F32),
             pltpu.VMEM((3, 16, 32, SLOTS), F32),
-            pltpu.VMEM((3, 128, SLOTS), F32),
+            pltpu.VMEM((2, 3, 128, SLOTS), F32),
             pltpu.VMEM((128, G), BF16),
             pltpu.VMEM((RANKS, G), BF16),
             pltpu.VMEM((6 * RANKS, G), BF16),
@@ -403,13 +422,13 @@
             pltpu.VMEM((4, 8, SLOTS), F32),
             pltpu.VMEM((N, 1, 128), F32),
             pltpu.VMEM((N, 1, 128), F32),
-            pltpu.VMEM((N, 4, 128), F32),
-            pltpu.VMEM((N, 4, 128), F32),
+            pltpu.VMEM((3 * N, 1, 128), F32),
+            pltpu.VMEM((3 * N, 1, 128), F32),
             pltpu.VMEM((16, N * 128), BF16),
             pltpu.VMEM((96, N * 128), BF16),
             pltpu.VMEM((128, N * 128), BF16),
             pltpu.VMEM((96, 128), F32),
-            dma, dma((4,)), dma((8,)), dma((8,)), dma, dma((4,)), dma, dma, dma,
+            dma((3,)), dma((4,)), dma((8,)), dma((8,)), dma, dma((4,)), dma, dma, dma,
         ],
         compiler_params=pltpu.CompilerParams(
             vmem_limit_bytes=67043328, collective_id=1, has_side_effects=True
@@ -418,7 +437,7 @@
     )(
         gather_blocks,
         gather_offsets,
-        photon_data.reshape(6, CX * CY, SLOTS),
+        photon_data,
         block_counts.T,
         albedo,
         gather_pixels.reshape(GROUPS, 128),

time: 49.6 us -> 47.7 us (0.962)
  Pallas kernels: 48 us -> 46.1 us
    pallas_call x1, Pallas kernels: 48 us -> 46.1 us  [per_device(): pl.pallas_call(kernel, out_shape=jax.ShapeDtypeStruct((3, 8, 256), F32),...]
where the time goes in v4:
time: 47.7 us; the launch traced here: 47.5 us
  Pallas kernels  46.1 us (97%)
  local copies, waits for them, and re-layouts  1.35 us (3%)
    pallas_call x1, Pallas kernels, per_device(): pl.pallas_call(kernel, out_shape=jax.ShapeDtypeStruct((3, 8, 256), F32),...  46.1 us
    unnamed x1, local copies, waits for them, and re-layouts  1.35 us

profile of v4, /device:TPU:1, one launch (start us, length us, event | category | flops | bytes accessed | tf_op | source)
XLA Modules:
  0.0 47.5 jit_solution(17245082385116835405)
XLA Ops:
  0.0 46.1 %photon_film.1 = f32[3,8,256]{2,1,0:T(8,128)} custom-call(s32[4,4096]{1,0:T(4,128)} %blocks.1, f32[3,4096]{1,0:T(4,128)} %goff.1, f32[6,64,32,128]{3,2,1,0:T(8,128)} %photons.1, s32[32,64]{1,0:T(8,128)} %bitcast.3, f32[3,4096]{1,0:T(4,128)} %alb.1, s32[32,128]{1,0:T(8,128)} %bitcast.4, s32[8,128]{1,0:T(8,128)} %bitcast.5), custom_call_target="tpu_custom_call" | custom-call | tf_op jit(solution)/shard_map/photon_film/pallas_call | solution.py:394
  46.1 1.3 %copy.9 = f32[3,8,256]{2,1,0:T(8,128)} copy(f32[3,8,256]{2,1,0:T(8,128)} %photon_film.1) | data formatting | bytes 49152

commit v5 on v4

--- a/solution.py
+++ b/solution.py
@@ -192,9 +192,11 @@
     psend.reshape(N, 128)[...] = by_owner(128.0 * part[:RANKS] + part[RANKS:])
 
 
-def weigh_tile(j, idx, off, table, prod, sums):
+def weigh_tile(j, idx, off, table, prod, sums, between):
     half = iota((8, SLOTS), 0) < 4
     for u in range(16):
+        if u in (2, 6, 10):
+            between(u // 4)
         g0 = j * 128 + 8 * u
         for pair in range(4):
             p, q = g0 + 2 * pair, g0 + 2 * pair + 1
@@ -214,11 +216,11 @@
             sums[c, 8 * u : 8 * u + 8, :] = (s[0] + s[1]) + (s[2] + s[3])
 
 
-def place_tile(j, alb, sums, rt, lhs):
+def place_tile(j, alb, sums, rt, lhs, channels=(0, 1, 2)):
     at = pl.ds(pl.multiple_of(j * 128, 128), 128)
     ones = jnp.ones((8, 256), BF16)
     place = rt[:, at]
-    for c in range(3):
+    for c in channels:
         whole = sums[c]
         high = whole.astype(BF16)
         low = (whole - high.astype(F32)).astype(BF16)
@@ -230,10 +232,13 @@
 
 def radiance(idx, off, table, prod, sums, alb, rt, lhs):
     def tiles(i, unused):
-        place_tile(jnp.maximum(2 * i - 1, 0), alb, sums.at[1], rt, lhs)
-        weigh_tile(2 * i, idx, off, table, prod, sums.at[0])
-        place_tile(2 * i, alb, sums.at[0], rt, lhs)
-        weigh_tile(2 * i + 1, idx, off, table, prod, sums.at[1])
+        for k in range(2):
+            j = 2 * i + k
+
+            def between(c):
+                place_tile(jnp.maximum(j - 1, 0), alb, sums.at[1 - k], rt, lhs, (c,))
+
+            weigh_tile(j, idx, off, table, prod, sums.at[k], between)
         return unused
 
     sums[...] = jnp.zeros((2, 3, 128, SLOTS), F32)

time: 47.7 us -> 47.4 us (level)
  no operation moved by 1% of the time
where the time goes in v5:
time: 47.4 us; the launch traced here: 47.1 us
  Pallas kernels  45.8 us (97%)
  local copies, waits for them, and re-layouts  1.35 us (3%)
    pallas_call x1, Pallas kernels, per_device(): pl.pallas_call(kernel, out_shape=jax.ShapeDtypeStruct((3, 8, 256), F32),...  45.8 us
    unnamed x1, local copies, waits for them, and re-layouts  1.35 us

profile of v5, /device:TPU:1, one launch (start us, length us, event | category | flops | bytes accessed | tf_op | source)
XLA Modules:
  0.0 47.1 jit_solution(12651954729388944007)
XLA Ops:
  0.0 45.8 %photon_film.1 = f32[3,8,256]{2,1,0:T(8,128)} custom-call(s32[4,4096]{1,0:T(4,128)} %blocks.1, f32[3,4096]{1,0:T(4,128)} %goff.1, f32[6,64,32,128]{3,2,1,0:T(8,128)} %photons.1, s32[32,64]{1,0:T(8,128)} %bitcast.3, f32[3,4096]{1,0:T(4,128)} %alb.1, s32[32,128]{1,0:T(8,128)} %bitcast.4, s32[8,128]{1,0:T(8,128)} %bitcast.5), custom_call_target="tpu_custom_call" | custom-call | tf_op jit(solution)/shard_map/photon_film/pallas_call | solution.py:399
  45.8 1.3 %copy.9 = f32[3,8,256]{2,1,0:T(8,128)} copy(f32[3,8,256]{2,1,0:T(8,128)} %photon_film.1) | data formatting | bytes 49152

commit v6 on v5

--- a/solution.py
+++ b/solution.py
@@ -232,17 +232,17 @@
 
 def radiance(idx, off, table, prod, sums, alb, rt, lhs):
     def tiles(i, unused):
-        for k in range(2):
-            j = 2 * i + k
+        for k in range(4):
+            j = 4 * i + k
 
             def between(c):
-                place_tile(jnp.maximum(j - 1, 0), alb, sums.at[1 - k], rt, lhs, (c,))
-
-            weigh_tile(j, idx, off, table, prod, sums.at[k], between)
+                place_tile(jnp.maximum(j - 1, 0), alb, sums.at[1 - k % 2], rt, lhs, (c,))
+
+            weigh_tile(j, idx, off, table, prod, sums.at[k % 2], between)
         return unused
 
     sums[...] = jnp.zeros((2, 3, 128, SLOTS), F32)
-    lax.fori_loop(0, GROUPS // 2, tiles, 0)
+    lax.fori_loop(0, GROUPS // 4, tiles, 0)
     place_tile(GROUPS - 1, alb, sums.at[1], rt, lhs)
 
 

time: 47.4 us -> 47 us (level)
  no operation moved by 1% of the time
where the time goes in v6:
time: 47 us; the launch traced here: 46.7 us
  Pallas kernels  45.4 us (97%)
  local copies, waits for them, and re-layouts  1.35 us (3%)
    pallas_call x1, Pallas kernels, per_device(): pl.pallas_call(kernel, out_shape=jax.ShapeDtypeStruct((3, 8, 256), F32),...  45.4 us
    unnamed x1, local copies, waits for them, and re-layouts  1.35 us

profile of v6, /device:TPU:1, one launch (start us, length us, event | category | flops | bytes accessed | tf_op | source)
XLA Modules:
  0.0 46.7 jit_solution(1252238519103928602)
XLA Ops:
  0.0 45.4 %photon_film.1 = f32[3,8,256]{2,1,0:T(8,128)} custom-call(s32[4,4096]{1,0:T(4,128)} %blocks.1, f32[3,4096]{1,0:T(4,128)} %goff.1, f32[6,64,32,128]{3,2,1,0:T(8,128)} %photons.1, s32[32,64]{1,0:T(8,128)} %bitcast.3, f32[3,4096]{1,0:T(4,128)} %alb.1, s32[32,128]{1,0:T(8,128)} %bitcast.4, s32[8,128]{1,0:T(8,128)} %bitcast.5), custom_call_target="tpu_custom_call" | custom-call | tf_op jit(solution)/shard_map/photon_film/pallas_call | solution.py:399
  45.4 1.3 %copy.9 = f32[3,8,256]{2,1,0:T(8,128)} copy(f32[3,8,256]{2,1,0:T(8,128)} %photon_film.1) | data formatting | bytes 49152
